TPU v7x, 32 devices: a whole 2x2x4 slice. The times are simulated.
32 devices in a mesh: dom: 8 (over y, x, core), tp: 4 (over z).
Axes of the slice: x: 2, y: 2, z: 4, core: 2. Of those that a mesh axis runs over, the one named last changes fastest.
Arguments:
- activations: bfloat16 [4, 128, 4096], P(None, 'dom', 'tp'), may hold values from -6 to 6
- norm_gain: float32 [4096], replicated, may hold values from 0.5 to 1.5
- w_query: bfloat16 [4096, 4096], P(None, 'tp'), may hold values from -0.09375 to 0.09375
- w_key: bfloat16 [4096, 1024], P(None, 'tp'), may hold values from -0.09375 to 0.09375
- value_weight: bfloat16 [4096, 1024], P(None, 'tp'), may hold values from -0.5 to 0.5
- w_output: bfloat16 [4096, 4096], P('tp'), may hold values from -0.09375 to 0.09375
- cache_keys: bfloat16 [128, 128, 1024], P('dom', None, 'tp'), may hold values from -740 to 740
- cache_values: bfloat16 [128, 128, 1024], P('dom', None, 'tp'), may hold values from -48 to 48
- tokens: int32 [4, 128], P(None, 'dom'), may hold values from 0 to 128255
- twisting_table: bfloat16 [128256], replicated, may hold values from -6 to 6
- twist_vec: float32 [4096], P('tp'), may hold values from -0.09375 to 0.09375
- previous_log_weights: float32 [128], P('dom'), may hold values from -300 to 0
- copy_counts: int32 [128], P('dom'), may hold values from 0 to 4, as said below
Outputs:
- attn_out: bfloat16 [4, 128, 4096], P(None, 'dom', 'tp')
- new_keys: bfloat16 [128, 132, 1024], P('dom', None, 'tp')
- new_values: bfloat16 [128, 132, 1024], P('dom', None, 'tp')
- out_logw: float32 [128], P('dom')
Inputs may be any that keep to these rules, and one draw needn't show every extreme that they name: copy_counts sum to 128; the particles of one index of dom have together at most 64 copies, and one index has exactly that many.
All inputs are finite; a program needn't handle non-finite values.
Results may differ from a plain program's by a relative error of at most 0.012.
The roundings to bfloat16 on the way count: a program that leaves them out, or rounds other values in their place, can miss the bound.
Values may be sent and summed in bfloat16 or wider, within the bound.
A program may use at most 128 MiB of HBM per device.

v0:
```python
import functools

import jax
import jax.numpy as jnp
import numpy as np
from jax import lax
from jax.experimental import pallas as pl
from jax.experimental.pallas import tpu as pltpu
from jax.sharding import PartitionSpec as P

D = 4096
HD = 128


def rotate(tensor, positions):
    middle = tensor.shape[-1] // 2
    frequency = 500000.0 ** (-2.0 * jnp.arange(middle, dtype=jnp.float32) / tensor.shape[-1])
    angles = positions[:, None] * frequency[None, :]
    cosine = jnp.cos(angles)[:, None, None, :]
    sine_part = jnp.sin(angles)[:, None, None, :]
    lower_half = tensor[..., :middle]
    upper_half = tensor[..., middle:]
    return jnp.concatenate(
        [
            lower_half * cosine - upper_half * sine_part,
            upper_half * cosine + lower_half * sine_part,
        ],
        -1,
    )


def local(
    activations,
    norm_gain,
    w_query,
    w_key,
    value_weight,
    w_output,
    cache_keys,
    cache_values,
    tokens,
    twisting_table,
    twist_vec,
    previous_log_weights,
    copy_counts,
):
    step_count = activations.shape[0]
    particle_count = activations.shape[1]
    span_old = cache_keys.shape[1]
    dom_size = lax.axis_size("dom")
    kv_local = w_key.shape[1] // HD
    q_local = w_query.shape[1] // HD
    group_size = q_local // kv_local
    all_counts = lax.all_gather(copy_counts, "dom", axis=0, tiled=True)
    copy_ends = jnp.cumsum(all_counts)
    ranks = jnp.arange(particle_count, dtype=jnp.int32) * dom_size + lax.axis_index("dom")
    ancestor = jnp.sum((copy_ends[None, :] <= ranks[:, None]).astype(jnp.int32), 1)
    all_keys = lax.all_gather(cache_keys, "dom", axis=0, tiled=True)
    all_values = lax.all_gather(cache_values, "dom", axis=0, tiled=True)

    gathered = lax.all_gather(activations, "tp", axis=2, tiled=True)
    inputs = gathered.astype(jnp.float32)
    normed = (
        inputs * lax.rsqrt(jnp.mean(inputs * inputs, -1, keepdims=True) + 1e-05) * norm_gain
    ).astype(jnp.bfloat16)
    flat_rows = normed.reshape(step_count * particle_count, D)
    positions = (span_old + jnp.arange(step_count, dtype=jnp.int32)).astype(jnp.float32)
    queries = jnp.dot(flat_rows, w_query, preferred_element_type=jnp.float32).reshape(
        step_count, particle_count, q_local, HD
    )
    queries = rotate(queries, positions).astype(jnp.bfloat16)
    fresh_keys = jnp.dot(flat_rows, w_key, preferred_element_type=jnp.float32).reshape(
        step_count, particle_count, kv_local, HD
    )
    fresh_keys = (
        rotate(fresh_keys, positions)
        .astype(jnp.bfloat16)
        .reshape(step_count, particle_count, kv_local * HD)
    )
    fresh_values = jnp.dot(flat_rows, value_weight, preferred_element_type=jnp.float32).astype(
        jnp.bfloat16
    )
    fresh_values = fresh_values.reshape(step_count, particle_count, kv_local * HD)
    fresh_keys = jnp.transpose(fresh_keys, (1, 0, 2))
    fresh_values = jnp.transpose(fresh_values, (1, 0, 2))
    key_rows = jnp.concatenate([cache_keys, fresh_keys], 1)
    value_rows = jnp.concatenate([cache_values, fresh_values], 1)
    key_span = span_old + step_count
    query_heads = queries.reshape(step_count, particle_count, kv_local, group_size, HD)
    key_heads = key_rows.reshape(particle_count, key_span, kv_local, HD)
    value_heads = value_rows.reshape(particle_count, key_span, kv_local, HD)
    scores = (
        jnp.einsum("snkgd,nlkd->snkgl", query_heads, key_heads, preferred_element_type=jnp.float32)
        / HD**0.5
    )
    allowed = (
        jnp.arange(key_span, dtype=jnp.int32)[None, :]
        <= (span_old + jnp.arange(step_count, dtype=jnp.int32))[:, None]
    )
    allowed = allowed[:, None, None, None, :]
    masked = jnp.where(allowed, scores, -jnp.inf)
    highest = jnp.max(masked, -1, keepdims=True)
    exponent = jnp.exp(masked - highest)
    weights = (exponent / jnp.sum(exponent, -1, keepdims=True)).astype(jnp.bfloat16)
    context = jnp.einsum(
        "snkgl,nlkd->snkgd", weights, value_heads, preferred_element_type=jnp.float32
    ).astype(jnp.bfloat16)
    context = context.reshape(step_count * particle_count, q_local * HD)
    partial_value = jnp.dot(context, w_output, preferred_element_type=jnp.float32).reshape(
        step_count, particle_count, D
    )
    head_mix = lax.psum_scatter(partial_value, "tp", scatter_dimension=2, tiled=True)
    attn_out = head_mix.astype(jnp.bfloat16)
    summed = activations.astype(jnp.float32) + head_mix
    aligned, energy = lax.psum(
        (jnp.sum(summed * twist_vec, -1), jnp.sum(summed * summed, -1)), "tp"
    )
    twisting_score = aligned / jnp.sqrt(energy / D + 1e-06)
    token_reward = twisting_table[tokens].astype(jnp.float32)
    particle_log_weight = previous_log_weights + jnp.sum(token_reward + twisting_score, 0)
    largest = lax.pmax(jnp.max(particle_log_weight), "dom")
    mass_total = lax.psum(jnp.sum(jnp.exp(particle_log_weight - largest)), "dom")
    out_logw = particle_log_weight - (largest + jnp.log(mass_total))
    fresh = lax.all_gather(
        jnp.concatenate([fresh_keys, fresh_values], 2), "dom", axis=0, tiled=True
    )[ancestor]
    width = fresh_keys.shape[2]
    new_keys = jnp.concatenate([all_keys[ancestor], fresh[..., :width]], 1)
    new_values = jnp.concatenate([all_values[ancestor], fresh[..., width:]], 1)
    return (attn_out, new_keys, new_values, out_logw)


MESH = pl.DeviceIdType.MESH


def layer_kernel(
    steps, parts, doms, tps,
    act, gain, wq, wk, wv, wo, ck, cv, twist, aux, cosine, sine,
    attn_out, all_k, all_v, fresh_sel, out_lw, anc_out,
    act_all, wq_v, wk_v, wv_v, wo_v, ck_v, cv_v, qs, cx, sc1, ctx_b, fresh, fresh_all,
    rs_send, rs_recv, sc_all, lw_all, cnt_all,
    loc, tp_send, tp_recv, dom_send, dom_recv, blk_send, blk_recv,
):
    f32, bf16 = jnp.float32, jnp.bfloat16
    me_d = lax.axis_index("dom")
    me_t = lax.axis_index("tp")
    rows, width = act.shape
    half = parts // 2
    kvw = wk.shape[1]
    groups = kvw // HD
    per = wq.shape[1] // kvw
    pack = steps * per
    c = me_d % 2
    x = (me_d // 2) % 2
    y = me_d // 4
    sib = me_d + 1 - 2 * c
    xn = me_d + 2 - 4 * x
    yn = me_d + 4 - 8 * y
    dn = xn + 4 - 8 * y

    barrier = pltpu.get_barrier_semaphore()
    for k in range(1, tps):
        pl.semaphore_signal(
            barrier, inc=1, device_id=(me_d, (me_t + k) % tps), device_id_type=MESH
        )
    for k in range(1, doms):
        pl.semaphore_signal(
            barrier, inc=1, device_id=((me_d + k) % doms, me_t), device_id_type=MESH
        )

    def fetch(i, src, dst):
        copy = pltpu.make_async_copy(src, dst, loc.at[i])
        copy.start()
        return copy

    own_act = fetch(0, act, act_all.at[me_t])
    load_q = fetch(1, wq, wq_v)
    load_k = fetch(2, wk, wk_v)
    load_v = fetch(3, wv, wv_v)
    load_ck = fetch(4, ck, ck_v)
    load_cv = fetch(5, cv, cv_v)
    load_o = fetch(6, wo, wo_v)

    cnt_all[me_d] = jnp.broadcast_to(aux[:, 1:], cnt_all.shape[1:])
    pl.semaphore_wait(barrier, tps + doms - 2)

    def tp_push(base, k, src, dst):
        copy = pltpu.make_async_remote_copy(
            src_ref=src, dst_ref=dst, send_sem=tp_send.at[base + k - 1],
            recv_sem=tp_recv.at[base + k - 1],
            device_id=(me_d, (me_t + k) % tps), device_id_type=MESH,
        )
        copy.start()
        return copy

    def dom_push(base, k, src, dst):
        copy = pltpu.make_async_remote_copy(
            src_ref=src, dst_ref=dst, send_sem=dom_send.at[base + k - 1],
            recv_sem=dom_recv.at[base + k - 1],
            device_id=((me_d + k) % doms, me_t), device_id_type=MESH,
        )
        copy.start()
        return copy

    acts = [tp_push(0, k, act, act_all.at[me_t]) for k in range(1, tps)]

    def piece(kind, to, which, h, slot, own):
        dst = (all_k, all_v)[which].at[slot, pl.ds(h * half, half)]
        src = (ck, cv)[which].at[pl.ds(h * half, half)] if own else dst
        i = kind * 4 + h * 2 + which
        copy = pltpu.make_async_remote_copy(
            src_ref=src, dst_ref=dst, send_sem=blk_send.at[i], recv_sem=blk_recv.at[i],
            device_id=(to, me_t), device_id_type=MESH,
        )
        copy.start()
        return copy

    moves = {}
    for h, kind, to in ((0, 0, xn), (1, 1, yn), (1, 0, xn), (0, 1, yn)):
        for which in range(2):
            moves[kind, h, which] = piece(kind, to, which, h, me_d, True)
    cnts = [dom_push(0, k, cnt_all.at[me_d], cnt_all.at[me_d]) for k in range(1, doms)]
    for h in range(2):
        for which in range(2):
            moves[3, h, which] = piece(3, sib, which, h, me_d, True)

    own_act.wait()
    for copy in acts:
        copy.wait()
    square = jnp.zeros((rows, 1), f32)
    for t in range(tps):
        u = act_all[t].astype(f32)
        square = square + jnp.sum(u * u, -1, keepdims=True)
    inv = lax.rsqrt(square / (width * tps) + 1e-05)
    normed = []
    for t in range(tps):
        u = act_all[t].astype(f32)
        normed.append((u * inv * gain[:, t * width : (t + 1) * width]).astype(bf16))

    def project(w):
        total = None
        for t in range(tps):
            part = jnp.dot(
                normed[t], w[t * width : (t + 1) * width, :], preferred_element_type=f32
            )
            total = part if total is None else total + part
        return total

    cos_t, sin_t = cosine[...], sine[...]

    def turn(u):
        return u * cos_t + pltpu.roll(u, HD // 2, 1) * sin_t

    load_k.wait()
    load_v.wait()
    keys = project(wk_v)
    for g in range(groups):
        fresh[:, g * HD : (g + 1) * HD] = turn(keys[:, g * HD : (g + 1) * HD]).astype(bf16)
    fresh[:, kvw:] = project(wv_v).astype(bf16)
    fresh_all[me_d] = fresh[...]
    news = [dom_push(doms - 1, k, fresh, fresh_all.at[me_d]) for k in range(1, doms)]
    load_q.wait()
    query = project(wq_v)
    for h in range(groups * per):
        g, j = h // per, h % per
        turned = turn(query[:, h * HD : (h + 1) * HD])
        for s in range(steps):
            qs[g, :, s * per + j, :] = turned[s * parts : (s + 1) * parts]
    load_ck.wait()
    load_cv.wait()
    put_k = fetch(7, ck_v, all_k.at[me_d])
    put_v = fetch(8, cv_v, all_v.at[me_d])

    lines = parts * pack
    row = lax.broadcasted_iota(jnp.int32, (lines, rows), 0)
    col = lax.broadcasted_iota(jnp.int32, (lines, rows), 1)
    allowed = (row // pack == col % parts) & (col // parts <= (row % pack) // per)
    scale = HD**0.5
    for g in range(groups):
        lanes = slice(g * HD, (g + 1) * HD)
        qg = qs[g].reshape(lines, HD).astype(bf16)
        for n in range(parts):
            sc1[g, n * pack : (n + 1) * pack, :] = lax.dot_general(
                qg[n * pack : (n + 1) * pack], ck_v[n, :, lanes],
                (((1,), (1,)), ((), ())), preferred_element_type=f32,
            )
        near = lax.dot_general(
            qg, fresh[:, lanes], (((1,), (1,)), ((), ())), preferred_element_type=f32
        )
        near = jnp.where(allowed, near / scale, -jnp.inf)
        far = sc1[g] / scale
        top = jnp.maximum(
            jnp.max(far, -1, keepdims=True), jnp.max(near, -1, keepdims=True)
        )
        far = jnp.exp(far - top)
        near = jnp.exp(near - top)
        mass = jnp.sum(far, -1, keepdims=True) + jnp.sum(near, -1, keepdims=True)
        far = (far / mass).astype(bf16)
        near = (near / mass).astype(bf16)
        extra = jnp.dot(
            near, fresh[:, kvw + g * HD : kvw + (g + 1) * HD], preferred_element_type=f32
        )
        for n in range(parts):
            span = slice(n * pack, (n + 1) * pack)
            cx[g, n] = extra[span] + jnp.dot(
                far[span], cv_v[n, :, lanes], preferred_element_type=f32
            )
    for h in range(groups * per):
        g, j = h // per, h % per
        for s in range(steps):
            ctx_b[s * parts : (s + 1) * parts, h * HD : (h + 1) * HD] = cx[
                g, :, s * per + j, :
            ].astype(bf16)
    load_o.wait()

    def mix(p):
        return jnp.dot(
            ctx_b[...], wo_v[:, pl.ds(pl.multiple_of(p * width, HD), width)],
            preferred_element_type=f32,
        )

    sums = []
    for k in range(1, tps):
        rs_send[k - 1] = mix((me_t + k) % tps)
        sums.append(tp_push(tps - 1, k, rs_send.at[k - 1], rs_recv.at[k - 1]))
    head = mix(me_t)

    def done(kind, h):
        for which in range(2):
            moves[kind, h, which].wait_recv()

    def relay(kind, to, h, slot):
        for which in range(2):
            moves[kind, h, which] = piece(kind, to, which, h, slot, False)

    done(0, 0)
    relay(2, yn, 0, xn)
    relay(4, sib, 0, xn)
    done(1, 1)
    relay(6, xn, 1, yn)
    relay(5, sib, 1, yn)
    for k in range(1, tps):
        sums[k - 1].wait()
        head = head + rs_recv[k - 1]
    attn_out[...] = head.astype(bf16)
    summed = act_all[me_t].astype(f32) + head
    along = jnp.sum(summed * twist[...], -1, keepdims=True)
    energy = jnp.sum(summed * summed, -1, keepdims=True)
    lane = lax.broadcasted_iota(jnp.int32, (rows, HD), 1)
    sc_all[me_t] = jnp.where(lane < HD // 2, along, energy)
    scores = [
        tp_push(2 * (tps - 1), k, sc_all.at[me_t], sc_all.at[me_t]) for k in range(1, tps)
    ]
    for copy in scores:
        copy.wait()
    both = sc_all[0]
    for t in range(1, tps):
        both = both + sc_all[t]
    score = both[:, :1] / jnp.sqrt(both[:, HD - 1 :] / (width * tps) + 1e-06)
    total = score[:parts]
    for s in range(1, steps):
        total = total + score[s * parts : (s + 1) * parts]
    mine = jnp.broadcast_to(aux[:, :1] + total, (parts, HD))
    lw_all[me_d] = mine
    lws = [
        dom_push(2 * (doms - 1), k, lw_all.at[me_d], lw_all.at[me_d]) for k in range(1, doms)
    ]

    done(0, 1)
    relay(4, sib, 1, xn)
    done(1, 0)
    relay(5, sib, 0, yn)

    for copy in cnts:
        copy.wait()
    for copy in news:
        copy.wait()
    whole = parts * doms
    number = cnt_all[...].reshape(whole, HD).astype(bf16)
    lower = lax.broadcasted_iota(jnp.int32, (whole, whole), 0)
    upper = lax.broadcasted_iota(jnp.int32, (whole, whole), 1)
    ends = jnp.dot(
        (upper <= lower).astype(f32).astype(bf16), number, preferred_element_type=f32
    )
    slot = lax.broadcasted_iota(jnp.int32, (whole, HD), 1)

    def ancestor(place):
        rank = (place * doms + me_d).astype(f32)
        return jnp.sum((ends <= rank).astype(f32), 0, keepdims=True).astype(jnp.int32)

    anc_out[...] = jnp.broadcast_to(ancestor(slot), anc_out.shape)
    lanes = lax.broadcasted_iota(jnp.int32, (1, HD), 1)
    wide = ancestor(slot // 8)
    target = (wide // parts) * rows + (lanes % 8) * parts + wide % parts
    target = jnp.where(lanes % 8 < steps, target, -1)
    index = lax.broadcasted_iota(jnp.int32, (doms * rows, HD), 0)
    pick = (index == target).astype(f32).astype(bf16)
    fresh_sel[...] = lax.dot_general(
        pick, fresh_all[...].reshape(doms * rows, 2 * kvw),
        (((0,), (0,)), ((), ())), preferred_element_type=f32,
    ).astype(bf16)

    for copy in lws:
        copy.wait()
    largest = jnp.max(lw_all[...], (0, 1), keepdims=True)[0]
    mass = jnp.sum(jnp.exp(lw_all[...] - largest[None]), (0, 1), keepdims=True)[0]
    out_lw[...] = mine - (largest + jnp.log(mass))

    done(2, 0)
    relay_d0 = [piece(7, sib, which, 0, dn, False) for which in range(2)]
    done(6, 1)
    relay_d1 = [piece(7, sib, which, 1, dn, False) for which in range(2)]
    for kind in (3, 4, 5):
        for h in range(2):
            done(kind, h)
    for copy in moves.values():
        copy.wait_send()
    for copy in relay_d0 + relay_d1:
        copy.wait()
    put_k.wait()
    put_v.wait()


def select_kernel(parts, steps, anc, fresh_sel, all_k, all_v, new_k, new_v, sem):
    span = all_k.shape[2]
    width = all_k.shape[3]
    copies = []
    for i in range(parts):
        a = anc[0, i]
        d, n = a // parts, a % parts
        for which, (src, dst) in enumerate(((all_k, new_k), (all_v, new_v))):
            copy = pltpu.make_async_copy(
                src.at[d, n], dst.at[i, pl.ds(0, span)], sem.at[2 * i + which]
            )
            copy.start()
            copies.append(copy)
    for i in range(parts):
        new_k[i, span:, :] = fresh_sel[i * 8 : i * 8 + steps, :width]
        new_v[i, span:, :] = fresh_sel[i * 8 : i * 8 + steps, width:]
    for copy in copies:
        copy.wait()


def fused(
    activations, norm_gain, w_query, w_key, value_weight, w_output, cache_keys, cache_values,
    tokens, twisting_table, twist_vec, previous_log_weights, copy_counts,
):
    f32, bf16 = jnp.float32, jnp.bfloat16
    steps, parts, width = activations.shape
    rows = steps * parts
    span = cache_keys.shape[1]
    kvw = w_key.shape[1]
    qw = w_query.shape[1]
    groups = kvw // HD
    pack = steps * (qw // kvw)
    doms = lax.axis_size("dom")
    tps = lax.axis_size("tp")
    middle = HD // 2
    angles = (span + np.arange(rows) // parts)[:, None] * (
        500000.0 ** (-2.0 * np.arange(middle) / HD)
    )
    cosine = np.concatenate([np.cos(angles)] * 2, 1).astype(np.float32)
    sine = np.concatenate([-np.sin(angles), np.sin(angles)], 1).astype(np.float32)
    reward = jnp.sum(twisting_table[tokens].astype(f32), 0)
    aux = jnp.stack([previous_log_weights + reward, copy_counts.astype(f32)], 1)
    vmem = pl.BlockSpec(memory_space=pltpu.VMEM)
    hbm = pl.BlockSpec(memory_space=pl.ANY)
    block = jax.ShapeDtypeStruct((doms,) + cache_keys.shape, bf16)
    attn, all_k, all_v, fresh_sel, out_lw, anc = pl.pallas_call(
        functools.partial(layer_kernel, steps, parts, doms, tps),
        out_shape=(
            jax.ShapeDtypeStruct((rows, width), bf16), block, block,
            jax.ShapeDtypeStruct((HD, 2 * kvw), bf16),
            jax.ShapeDtypeStruct((parts, HD), f32),
            jax.ShapeDtypeStruct((8, HD), jnp.int32),
        ),
        in_specs=[hbm, vmem] + [hbm] * 6 + [vmem] * 4,
        out_specs=(vmem, hbm, hbm, vmem, vmem, vmem),
        scratch_shapes=[
            pltpu.VMEM((tps, rows, width), bf16),
            pltpu.VMEM(w_query.shape, bf16),
            pltpu.VMEM(w_key.shape, bf16),
            pltpu.VMEM(value_weight.shape, bf16),
            pltpu.VMEM(w_output.shape, bf16),
            pltpu.VMEM(cache_keys.shape, bf16),
            pltpu.VMEM(cache_values.shape, bf16),
            pltpu.VMEM((groups, parts, pack, HD), f32),
            pltpu.VMEM((groups, parts, pack, HD), f32),
            pltpu.VMEM((groups, parts * pack, span), f32),
            pltpu.VMEM((rows, qw), bf16),
            pltpu.VMEM((rows, 2 * kvw), bf16),
            pltpu.VMEM((doms, rows, 2 * kvw), bf16),
            pltpu.VMEM((tps - 1, rows, width), f32),
            pltpu.VMEM((tps - 1, rows, width), f32),
            pltpu.VMEM((tps, rows, HD), f32),
            pltpu.VMEM((doms, parts, HD), f32),
            pltpu.VMEM((doms, parts, HD), f32),
            pltpu.SemaphoreType.DMA((9,)),
            pltpu.SemaphoreType.DMA((3 * (tps - 1),)),
            pltpu.SemaphoreType.DMA((3 * (tps - 1),)),
            pltpu.SemaphoreType.DMA((3 * (doms - 1),)),
            pltpu.SemaphoreType.DMA((3 * (doms - 1),)),
            pltpu.SemaphoreType.DMA((32,)),
            pltpu.SemaphoreType.DMA((32,)),
        ],
        compiler_params=pltpu.CompilerParams(
            collective_id=0, has_side_effects=True, vmem_limit_bytes=56 << 20
        ),
        name="layer",
    )(
        activations.reshape(rows, width), norm_gain.reshape(1, -1), w_query, w_key,
        value_weight, w_output, cache_keys, cache_values, twist_vec.reshape(1, -1), aux,
        jnp.asarray(cosine), jnp.asarray(sine),
    )
    result = jax.ShapeDtypeStruct((parts, span + steps, kvw), bf16)
    new_k, new_v = pl.pallas_call(
        functools.partial(select_kernel, parts, steps),
        out_shape=(result, result),
        in_specs=[pl.BlockSpec(memory_space=pltpu.SMEM), vmem, hbm, hbm],
        out_specs=(vmem, vmem),
        scratch_shapes=[pltpu.SemaphoreType.DMA((2 * parts,))],
        name="select",
    )(anc, fresh_sel, all_k, all_v)
    return attn.reshape(steps, parts, width), new_k, new_v, out_lw[:, 0]


def solution(mesh):
    body = fused if mesh.shape["dom"] == 8 else local
    return jax.shard_map(
        body,
        mesh=mesh,
        in_specs=(
            P(None, "dom", "tp"),
            P(),
            P(None, "tp"),
            P(None, "tp"),
            P(None, "tp"),
            P("tp", None),
            P("dom", None, "tp"),
            P("dom", None, "tp"),
            P(None, "dom"),
            P(),
            P("tp"),
            P("dom"),
            P("dom"),
        ),
        out_specs=(P(None, "dom", "tp"), P("dom", None, "tp"), P("dom", None, "tp"), P("dom")),
        check_vma=False,
    )
```

profile of v0, /device:TPU:0, one launch (start us, length us, event | category | flops | bytes accessed | tf_op | source)
XLA Modules:
  0.0 103.5 jit_solution(16041607396230409005)
XLA Ops:
  0.6 0.0 copy-start
  0.6 0.7 convert_bitcast_fusion
  1.3 0.7 compare_select_fusion
  2.0 0.1 reshape.26
  2.1 0.0 copy-done
  2.1 0.8 gather_fusion
  2.9 0.1 reshape.34
  3.0 0.7 add_bitcast_fusion
  3.7 0.7 copy.27.aux
  4.4 89.2 %layer.1 = (bf16[64,1024]{1,0:T(8,128)(2,1)}, bf16[8,16,128,256]{3,2,1,0:T(8,128)(2,1)}, bf16[8,16,128,256]{3,2,1,0:T(8,128)(2,1)}, bf16[128,512]{1,0:T(8,128)(2...) custom-call(bf16[64,1024]{1,0:T(8,128)(2,1)} %bitcast.8, f32[1,4096]{1,0:T(1,128)} %bitcast.10, bf16[4096,1024]{1,0:T(8,128)(2,1)} %wq.1, ...), custom_call_target="tpu_custom_call" | custom-call | tf_op jit(solution)/shard_map/layer/pallas_call | solution.py:469
  93.6 1.3 %slice_reduce_fusion = f32[16]{0:T(128)} fusion(f32[16,128]{1,0:T(8,128)} %get-tuple-element.19), kind=kLoop, calls=%fused_computation.1 | loop fusion | bytes 128 | tf_op jit(solution)/shard_map/slice | solution.py:524
  94.9 4.2 %select.1 = (bf16[16,132,256]{2,1,0:T(8,128)(2,1)}, bf16[16,132,256]{2,1,0:T(8,128)(2,1)}) custom-call(s32[8,128]{1,0:T(8,128)} %get-tuple-element.13.anc, bf16[128,512]{1,0:T(8,128)(2,1)} %get-tuple-element.14.fresh_sel, bf16[8,16,128,256]{3,2,1,0:T(8,128)(2,1)} %get-tuple-element.15.all_k, bf16[8,16,128,256]{3,2,1,0:T(8,128)(2,1)} %get-tuple-element.16.all_v), custom_call_target="tpu_custom_call" | custom-call | tf_op jit(solution)/shard_map/select/pallas_call | solution.py:516
  99.1 0.0 copy-start.1
  99.1 0.0 copy-start.2
  99.1 2.5 %copy.28 = bf16[16,132,256]{2,0,1:T(8,128)(2,1)} copy(bf16[16,132,256]{2,1,0:T(8,128)(2,1)} %get-tuple-element.29) | data formatting | bytes 2162688
  101.7 0.0 copy-done.1
  101.7 1.2 %copy.29 = bf16[16,132,256]{2,0,1:T(8,128)(2,1)} copy(bf16[16,132,256]{2,1,0:T(8,128)(2,1)S(1)} %copy-done.1) | data formatting | bytes 2162688
  102.9 0.0 copy-done.2
  102.9 0.7 copy.31
  (3 shorter events, 0.0 us)
Async XLA Ops:
  0.6 1.5 %copy-start = (bf16[128256]{0:T(1024)(128)(2,1)S(1)}, bf16[128256]{0:T(1024)(128)(2,1)}, u32[]{:S(2)}) copy-start(bf16[128256]{0:T(1024)(128)(2,1)} %param.24) | copy-start | bytes 769540
  99.1 2.6 %copy-start.1 = (bf16[16,132,256]{2,1,0:T(8,128)(2,1)S(1)}, bf16[16,132,256]{2,1,0:T(8,128)(2,1)}, u32[]{:S(2)}) copy-start(bf16[16,132,256]{2,1,0:T(8,128)(2,1)} %get-tuple-element.30) | copy-start | bytes 3244036
  99.1 3.7 %copy-start.2 = (bf16[64,1024]{1,0:T(8,128)(2,1)S(1)}, bf16[64,1024]{1,0:T(8,128)(2,1)}, u32[]{:S(2)}) copy-start(bf16[64,1024]{1,0:T(8,128)(2,1)} %get-tuple-element.12) | copy-start | bytes 393220
where the time goes:
time: 104 us
  Pallas kernels  93.4 us (90%)
  local copies, waits for them, and re-layouts  7.38 us (7%)
  other arithmetic  2.09 us (2%)
    pallas_call x1, Pallas kernels, fused(): pl.pallas_call(functools.partial(layer_kernel, steps, parts, doms, tps),...  89.2 us
    unnamed x9, local copies, waits for them, and re-layouts  4.4 us
    pallas_call x1, Pallas kernels, fused(): pl.pallas_call(functools.partial(select_kernel, parts, steps), out_shape=...  4.17 us

commit v1 on v0

--- a/solution.py
+++ b/solution.py
@@ -10,6 +10,7 @@
 
 D = 4096
 HD = 128
+CAP = 8
 
 
 def rotate(tensor, positions):
@@ -441,31 +442,21 @@
         copy.wait()
 
 
-def fused(
-    activations, norm_gain, w_query, w_key, value_weight, w_output, cache_keys, cache_values,
-    tokens, twisting_table, twist_vec, previous_log_weights, copy_counts,
+def all_rows(
+    steps, parts, act, gain, wq, wk, wv, wo, ck, cv, twist, aux, cosine, sine,
 ):
     f32, bf16 = jnp.float32, jnp.bfloat16
-    steps, parts, width = activations.shape
-    rows = steps * parts
-    span = cache_keys.shape[1]
-    kvw = w_key.shape[1]
-    qw = w_query.shape[1]
+    rows, width = act.shape
+    span = ck.shape[1]
+    kvw = wk.shape[1]
+    qw = wq.shape[1]
     groups = kvw // HD
     pack = steps * (qw // kvw)
     doms = lax.axis_size("dom")
     tps = lax.axis_size("tp")
-    middle = HD // 2
-    angles = (span + np.arange(rows) // parts)[:, None] * (
-        500000.0 ** (-2.0 * np.arange(middle) / HD)
-    )
-    cosine = np.concatenate([np.cos(angles)] * 2, 1).astype(np.float32)
-    sine = np.concatenate([-np.sin(angles), np.sin(angles)], 1).astype(np.float32)
-    reward = jnp.sum(twisting_table[tokens].astype(f32), 0)
-    aux = jnp.stack([previous_log_weights + reward, copy_counts.astype(f32)], 1)
     vmem = pl.BlockSpec(memory_space=pltpu.VMEM)
     hbm = pl.BlockSpec(memory_space=pl.ANY)
-    block = jax.ShapeDtypeStruct((doms,) + cache_keys.shape, bf16)
+    block = jax.ShapeDtypeStruct((doms,) + ck.shape, bf16)
     attn, all_k, all_v, fresh_sel, out_lw, anc = pl.pallas_call(
         functools.partial(layer_kernel, steps, parts, doms, tps),
         out_shape=(
@@ -478,12 +469,12 @@
         out_specs=(vmem, hbm, hbm, vmem, vmem, vmem),
         scratch_shapes=[
             pltpu.VMEM((tps, rows, width), bf16),
-            pltpu.VMEM(w_query.shape, bf16),
-            pltpu.VMEM(w_key.shape, bf16),
-            pltpu.VMEM(value_weight.shape, bf16),
-            pltpu.VMEM(w_output.shape, bf16),
-            pltpu.VMEM(cache_keys.shape, bf16),
-            pltpu.VMEM(cache_values.shape, bf16),
+            pltpu.VMEM(wq.shape, bf16),
+            pltpu.VMEM(wk.shape, bf16),
+            pltpu.VMEM(wv.shape, bf16),
+            pltpu.VMEM(wo.shape, bf16),
+            pltpu.VMEM(ck.shape, bf16),
+            pltpu.VMEM(cv.shape, bf16),
             pltpu.VMEM((groups, parts, pack, HD), f32),
             pltpu.VMEM((groups, parts, pack, HD), f32),
             pltpu.VMEM((groups, parts * pack, span), f32),
@@ -504,14 +495,10 @@
             pltpu.SemaphoreType.DMA((32,)),
         ],
         compiler_params=pltpu.CompilerParams(
-            collective_id=0, has_side_effects=True, vmem_limit_bytes=56 << 20
+            collective_id=4, has_side_effects=True, vmem_limit_bytes=56 << 20
         ),
         name="layer",
-    )(
-        activations.reshape(rows, width), norm_gain.reshape(1, -1), w_query, w_key,
-        value_weight, w_output, cache_keys, cache_values, twist_vec.reshape(1, -1), aux,
-        jnp.asarray(cosine), jnp.asarray(sine),
-    )
+    )(act, gain, wq, wk, wv, wo, ck, cv, twist, aux, cosine, sine)
     result = jax.ShapeDtypeStruct((parts, span + steps, kvw), bf16)
     new_k, new_v = pl.pallas_call(
         functools.partial(select_kernel, parts, steps),
@@ -521,11 +508,570 @@
         scratch_shapes=[pltpu.SemaphoreType.DMA((2 * parts,))],
         name="select",
     )(anc, fresh_sel, all_k, all_v)
+    return attn, new_k, new_v, out_lw
+
+
+def plan_kernel(parts, doms, cap, steps, rows, cnt, tab, cnt_all, send, recv):
+    f32, bf16, i32 = jnp.float32, jnp.bfloat16, jnp.int32
+    me_d = lax.axis_index("dom")
+    me_t = lax.axis_index("tp")
+    core = me_d % 2
+    x = (me_d // 2) % 2
+    y = me_d // 4
+    chip = me_d // 2
+    barrier = pltpu.get_barrier_semaphore()
+    for k in range(1, doms):
+        pl.semaphore_signal(
+            barrier, inc=1, device_id=((me_d + k) % doms, me_t), device_id_type=MESH
+        )
+    cnt_all[me_d] = jnp.zeros(cnt_all.shape[1:], f32)
+    cnt_all[me_d, :, :parts] = jnp.broadcast_to(cnt[...].astype(f32), (8, parts))
+    pl.semaphore_wait(barrier, doms - 1)
+    copies = []
+    for k in range(1, doms):
+        copy = pltpu.make_async_remote_copy(
+            src_ref=cnt_all.at[me_d], dst_ref=cnt_all.at[me_d],
+            send_sem=send.at[k - 1], recv_sem=recv.at[k - 1],
+            device_id=((me_d + k) % doms, me_t), device_id_type=MESH,
+        )
+        copy.start()
+        copies.append(copy)
+    for copy in copies:
+        copy.wait()
+    whole = parts * doms
+    j = lax.broadcasted_iota(i32, (whole, HD), 0)
+    lane = lax.broadcasted_iota(i32, (whole, HD), 1)
+    spread = jnp.concatenate([cnt_all[d] for d in range(doms) for _ in range(parts // 8)], 0)
+    column = jnp.sum(jnp.where(lane == j % parts, spread, 0.0), -1, keepdims=True)
+    number = jnp.broadcast_to(column, (whole, HD))
+    first = lax.broadcasted_iota(i32, (whole, whole), 0)
+    second = lax.broadcasted_iota(i32, (whole, whole), 1)
+
+    def total(mask, values):
+        return jnp.dot(
+            mask.astype(f32).astype(bf16), values.astype(bf16), preferred_element_type=f32
+        )
+
+    ends = total(second <= first, number)
+    loads = total(second // parts == first // parts, number)
+    number = number.astype(i32)
+    ends = ends.astype(i32)
+    starts = ends - number
+    top = jnp.max(loads, (0, 1), keepdims=True)
+    owner = j // parts
+    heavy = jnp.min(jnp.where(loads == top, owner, doms).astype(f32), (0, 1), keepdims=True)
+    heavy = heavy.astype(i32)
+    light = owner != heavy
+    home = j // (2 * parts)
+
+    def needs(to):
+        hit = None
+        for m in range(4):
+            one = (m < number) & (((starts + m) % doms) // 2 == to)
+            hit = one if hit is None else hit | one
+        return hit & light & (home != to)
+
+    kind = (lane // cap) % 4
+    there_x = x + kind % 2 - 2 * x * (kind % 2)
+    there_y = y + kind // 2 - 2 * y * (kind // 2)
+    need_send = needs(2 * there_y + there_x)
+    need_here = needs(jnp.broadcast_to(chip, (whole, HD)))
+    need_any = needs(lane % 4)
+    before = (second < first) & (second // (2 * parts) == first // (2 * parts))
+    places = total(
+        before,
+        jnp.concatenate([u.astype(f32) for u in (need_send, need_here, need_any)], 1),
+    ).astype(i32)
+    place_send = places[:, :HD]
+    place_here = places[:, HD : 2 * HD]
+    place_any = places[:, 2 * HD :]
+    local_row = j % parts + parts * (owner % 2 + core - 2 * core * (owner % 2))
+    picked = need_send & (place_send == lane % cap) & (home == chip)
+    sources = jnp.sum(jnp.where(picked, local_row, 0).astype(f32), 0, keepdims=True)
+    hx, hy = home % 2, home // 2
+    away = (hx + x - 2 * x * hx) + 2 * (hy + y - 2 * y * hy)
+    value = jnp.where(
+        away == 0,
+        local_row,
+        jnp.where(light, 3 * parts + (away - 1) * cap + place_here, 2 * parts + j % parts),
+    )
+    rank = lane * doms + me_d
+    mine = (starts <= rank) & (rank < ends)
+    index = jnp.sum(jnp.where(mine, value, 0).astype(f32), 0, keepdims=True)
+    wide = (lane // 8) * doms + me_d
+    old = jnp.sum((ends <= wide).astype(f32), 0, keepdims=True).astype(i32)
+    row = lax.broadcasted_iota(i32, (1, HD), 1)
+    target = (old // parts) * rows + (row % 8) * parts + old % parts
+    target = jnp.where(row % 8 < steps, target, -1)
+    longest = jnp.max(
+        jnp.where(need_any, place_any + 1, 0).astype(f32), (0, 1), keepdims=True
+    ).astype(i32)
+    base = parts * (heavy % 2 + core - 2 * core * (heavy % 2))
+    branch = jnp.where(longest <= cap, heavy // 2, 4)
+    tab[0:1, :] = sources.astype(i32)
+    tab[1:2, :] = index.astype(i32)
+    tab[2:3, :] = jnp.broadcast_to(base, (1, HD))
+    tab[3:4, :] = target
+    tab[4:5, :] = jnp.broadcast_to(branch, (1, HD))
+    tab[5:8, :] = jnp.zeros((3, HD), i32)
+
+
+def main_kernel(
+    steps, parts, doms, tps, cap, hot,
+    act, gain, wq, wk, wv, wo, ck, cv, twist, aux, cosine, sine, tab, tabv,
+    attn_out, new_k, new_v, out_lw,
+    act_all, wq_v, wk_v, wv_v, wo_v, chip_k, chip_v, all_k, all_v, send_k, send_v,
+    qs, cx, sc1, ctx_b, fresh_all, rs_send, rs_recv, sc_all, lw_all,
+    loc, tp_send, tp_recv, lw_send, lw_recv, sib_send, sib_recv,
+    hv_send, hv_recv, li_send, li_recv, fr_send, fr_recv,
+):
+    f32, bf16 = jnp.float32, jnp.bfloat16
+    me_d = lax.axis_index("dom")
+    me_t = lax.axis_index("tp")
+    rows, width = act.shape
+    kvw = wk.shape[1]
+    groups = kvw // HD
+    per = wq.shape[1] // kvw
+    pack = steps * per
+    span = ck.shape[1]
+    c = me_d % 2
+    x = (me_d // 2) % 2
+    y = me_d // 4
+    sib = me_d + 1 - 2 * c
+    xn = me_d + 2 - 4 * x
+    yn = me_d + 4 - 8 * y
+    dn = xn + 4 - 8 * y
+    rx = x if hot % 2 == 0 else 1 - x
+    ry = y if hot // 2 == 0 else 1 - y
+    pos = (1 - c) * (3 * ry + rx * (1 - 2 * ry)) + c * (3 * rx + ry * (1 - 2 * rx))
+    turn_y = (pos + c) % 2
+    onward = xn + turn_y * (yn - xn)
+
+    barrier = pltpu.get_barrier_semaphore()
+    for k in range(1, tps):
+        pl.semaphore_signal(
+            barrier, inc=1, device_id=(me_d, (me_t + k) % tps), device_id_type=MESH
+        )
+    for k in range(1, doms):
+        pl.semaphore_signal(
+            barrier, inc=1, device_id=((me_d + k) % doms, me_t), device_id_type=MESH
+        )
+
+    def fetch(i, src, dst):
+        copy = pltpu.make_async_copy(src, dst, loc.at[i])
+        copy.start()
+        return copy
+
+    own_act = fetch(0, act, act_all.at[me_t])
+    load_ck = fetch(4, ck, chip_k.at[pl.ds(0, parts)])
+    load_cv = fetch(5, cv, chip_v.at[pl.ds(0, parts)])
+    load_k = fetch(2, wk, wk_v)
+    load_v = fetch(3, wv, wv_v)
+    load_q = fetch(1, wq, wq_v)
+    load_o = fetch(6, wo, wo_v)
+    pl.semaphore_wait(barrier, tps + doms - 2)
+
+    def push(src, dst, ssem, rsem, to_d, to_t):
+        return pltpu.make_async_remote_copy(
+            src_ref=src, dst_ref=dst, send_sem=ssem, recv_sem=rsem,
+            device_id=(to_d, to_t), device_id_type=MESH,
+        )
+
+    def tp_push(base, k, src, dst):
+        copy = push(
+            src, dst, tp_send.at[base + k - 1], tp_recv.at[base + k - 1],
+            me_d, (me_t + k) % tps,
+        )
+        copy.start()
+        return copy
+
+    acts = [tp_push(0, k, act, act_all.at[me_t]) for k in range(1, tps)]
+    swaps = []
+    for i, (src, dst) in enumerate(((ck, chip_k), (cv, chip_v))):
+        copy = push(src, dst.at[pl.ds(parts, parts)], sib_send.at[i], sib_recv.at[i], sib, me_t)
+        copy.start()
+        swaps.append(copy)
+
+    lane_rows = cap // 2
+    hot_rows = parts // 2
+    chunk = hot_rows // 4
+
+    def hot_copy(q, which, to, base):
+        ref = (all_k, all_v)[which]
+        area = ref.at[pl.ds(2 * parts + hot_rows * c + q * chunk, chunk)]
+        i = base + q * 2 + which
+        return push(area, area, hv_send.at[i], hv_recv.at[i], to, me_t)
+
+    def forward(q, which):
+        return hot_copy(q, which, onward, 0)
+
+    def mirror(q, which):
+        return hot_copy(q, which, sib, 8)
+
+    def light_area(ref, k):
+        return ref.at[pl.ds(3 * parts + (k - 1) * cap + lane_rows * c, lane_rows)]
+
+    def light(k, which):
+        i = (k - 1) * 2 + which
+        return push(
+            (send_k, send_v)[which].at[k - 1], light_area((all_k, all_v)[which], k),
+            li_send.at[i], li_recv.at[i], (xn, yn, dn)[k - 1], me_t,
+        )
+
+    def light_mirror(k, which):
+        i = 6 + (k - 1) * 2 + which
+        area = light_area((all_k, all_v)[which], k)
+        return push(area, area, li_send.at[i], li_recv.at[i], sib, me_t)
+
+    load_ck.wait()
+    load_cv.wait()
+    for copy in swaps:
+        copy.wait()
+    both_k = fetch(7, chip_k, all_k.at[pl.ds(0, 2 * parts)])
+    both_v = fetch(8, chip_v, all_v.at[pl.ds(0, 2 * parts)])
+
+    @pl.when(pos == 0)
+    def _():
+        for i in range(hot_rows):
+            at = tab[2, 0] + hot_rows * c + i
+            all_k[2 * parts + hot_rows * c + i] = chip_k[at]
+            all_v[2 * parts + hot_rows * c + i] = chip_v[at]
+            if i % chunk == chunk - 1:
+                for which in range(2):
+                    forward(i // chunk, which).start()
+
+    for k in (3, 1, 2):
+        for t in range(lane_rows):
+            at = tab[0, k * cap + lane_rows * c + t]
+            send_k[k - 1, t] = chip_k[at]
+            send_v[k - 1, t] = chip_v[at]
+        for which in range(2):
+            light(k, which).start()
+
+    def relay(*list_of):
+        for where, q in list_of:
+
+            @pl.when(pos == where)
+            def _():
+                for which in range(2):
+                    forward(q, which).wait_recv()
+                    if where < 3:
+                        forward(q, which).start()
+                    mirror(q, which).start()
+
+    own_act.wait()
+    for copy in acts:
+        copy.wait()
+    square = jnp.zeros((rows, 1), f32)
+    for t in range(tps):
+        u = act_all[t].astype(f32)
+        square = square + jnp.sum(u * u, -1, keepdims=True)
+    inv = lax.rsqrt(square / (width * tps) + 1e-05)
+    normed = []
+    for t in range(tps):
+        u = act_all[t].astype(f32)
+        normed.append((u * inv * gain[:, t * width : (t + 1) * width]).astype(bf16))
+
+    def project(w):
+        total = None
+        for t in range(tps):
+            part = jnp.dot(
+                normed[t], w[t * width : (t + 1) * width, :], preferred_element_type=f32
+            )
+            total = part if total is None else total + part
+        return total
+
+    cos_t, sin_t = cosine[...], sine[...]
+
+    def turn(u):
+        return u * cos_t + pltpu.roll(u, HD // 2, 1) * sin_t
+
+    load_k.wait()
+    load_v.wait()
+    keys = project(wk_v)
+    fresh = fresh_all.at[me_d]
+    for g in range(groups):
+        fresh[:, g * HD : (g + 1) * HD] = turn(keys[:, g * HD : (g + 1) * HD]).astype(bf16)
+    fresh[:, kvw:] = project(wv_v).astype(bf16)
+
+    def fresh_copy(i, block, to):
+        area = fresh_all.at[block]
+        return push(area, area, fr_send.at[i], fr_recv.at[i], to, me_t)
+
+    news = [fresh_copy(i, me_d, to) for i, to in enumerate((dn, xn, yn, sib))]
+    for copy in news:
+        copy.start()
+    load_q.wait()
+    query = project(wq_v)
+    for h in range(groups * per):
+        g, j = h // per, h % per
+        turned = turn(query[:, h * HD : (h + 1) * HD])
+        for s in range(steps):
+            qs[g, :, s * per + j, :] = turned[s * parts : (s + 1) * parts]
+    relay((1, 0))
+
+    lines = parts * pack
+    row = lax.broadcasted_iota(jnp.int32, (lines, rows), 0)
+    col = lax.broadcasted_iota(jnp.int32, (lines, rows), 1)
+    allowed = (row // pack == col % parts) & (col // parts <= (row % pack) // per)
+    scale = HD**0.5
+    for g in range(groups):
+        lanes = slice(g * HD, (g + 1) * HD)
+        qg = qs[g].reshape(lines, HD).astype(bf16)
+        for n in range(parts):
+            sc1[g, n * pack : (n + 1) * pack, :] = lax.dot_general(
+                qg[n * pack : (n + 1) * pack], chip_k[n, :, lanes],
+                (((1,), (1,)), ((), ())), preferred_element_type=f32,
+            )
+        near = lax.dot_general(
+            qg, fresh[:, lanes], (((1,), (1,)), ((), ())), preferred_element_type=f32
+        )
+        near = jnp.where(allowed, near / scale, -jnp.inf)
+        far = sc1[g] / scale
+        top = jnp.maximum(
+            jnp.max(far, -1, keepdims=True), jnp.max(near, -1, keepdims=True)
+        )
+        far = jnp.exp(far - top)
+        near = jnp.exp(near - top)
+        mass = jnp.sum(far, -1, keepdims=True) + jnp.sum(near, -1, keepdims=True)
+        far = (far / mass).astype(bf16)
+        near = (near / mass).astype(bf16)
+        extra = jnp.dot(
+            near, fresh[:, kvw + g * HD : kvw + (g + 1) * HD], preferred_element_type=f32
+        )
+        for n in range(parts):
+            part = slice(n * pack, (n + 1) * pack)
+            cx[g, n] = extra[part] + jnp.dot(
+                far[part], chip_v[n, :, lanes], preferred_element_type=f32
+            )
+        if g == 0:
+            relay((1, 1), (2, 0))
+    for h in range(groups * per):
+        g, j = h // per, h % per
+        for s in range(steps):
+            ctx_b[s * parts : (s + 1) * parts, h * HD : (h + 1) * HD] = cx[
+                g, :, s * per + j, :
+            ].astype(bf16)
+    relay((1, 2), (2, 1), (3, 0))
+    load_o.wait()
+
+    def mix(p):
+        return jnp.dot(
+            ctx_b[...], wo_v[:, pl.ds(pl.multiple_of(p * width, HD), width)],
+            preferred_element_type=f32,
+        )
+
+    sums = []
+    for k in (2, 1, 3)[: tps - 1]:
+        rs_send[k - 1] = mix((me_t + k) % tps).astype(bf16)
+        sums.append(tp_push(tps - 1, k, rs_send.at[k - 1], rs_recv.at[k - 1]))
+    head = mix(me_t)
+    relay((1, 3), (2, 2), (3, 1))
+    for copy in news:
+        copy.wait_recv()
+    passed = [fresh_copy(4 + i, b + c, sib) for i, b in enumerate((dn - c, xn - c, yn - c))]
+    for copy in passed:
+        copy.start()
+    for copy in sums:
+        copy.wait()
+    for k in range(1, tps):
+        head = head + rs_recv[k - 1].astype(f32)
+    attn_out[...] = head.astype(bf16)
+    summed = act_all[me_t].astype(f32) + head
+    along = jnp.sum(summed * twist[...], -1, keepdims=True)
+    energy = jnp.sum(summed * summed, -1, keepdims=True)
+    lane = lax.broadcasted_iota(jnp.int32, (rows, HD), 1)
+    sc_all[me_t] = jnp.where(lane < HD // 2, along, energy)
+    scores = [
+        tp_push(2 * (tps - 1), k, sc_all.at[me_t], sc_all.at[me_t]) for k in range(1, tps)
+    ]
+    relay((2, 3), (3, 2))
+    for copy in scores:
+        copy.wait()
+    both = sc_all[0]
+    for t in range(1, tps):
+        both = both + sc_all[t]
+    score = both[:, :1] / jnp.sqrt(both[:, HD - 1 :] / (width * tps) + 1e-06)
+    total = score[:parts]
+    for s in range(1, steps):
+        total = total + score[s * parts : (s + 1) * parts]
+    mine = jnp.broadcast_to(aux[...] + total, (parts, HD))
+    lw_all[me_d] = mine
+    lws = []
+    for k in range(1, doms):
+        copy = push(
+            lw_all.at[me_d], lw_all.at[me_d], lw_send.at[k - 1], lw_recv.at[k - 1],
+            (me_d + k) % doms, me_t,
+        )
+        copy.start()
+        lws.append(copy)
+
+    for k in (1, 2, 3):
+        for which in range(2):
+            light(k, which).wait_recv()
+            light_mirror(k, which).start()
+    relay((3, 3))
+    for copy in passed:
+        copy.wait()
+    index = lax.broadcasted_iota(jnp.int32, (doms * rows, HD), 0)
+    pick = (index == tabv[3:4, :]).astype(f32).astype(bf16)
+    chosen = lax.dot_general(
+        pick, fresh_all[...].reshape(doms * rows, 2 * kvw),
+        (((0,), (0,)), ((), ())), preferred_element_type=f32,
+    ).astype(bf16)
+    for i in range(parts):
+        new_k[i, span:, :] = chosen[i * 8 : i * 8 + steps, :kvw]
+        new_v[i, span:, :] = chosen[i * 8 : i * 8 + steps, kvw:]
+
+    for copy in lws:
+        copy.wait()
+    largest = jnp.max(lw_all[...], (0, 1), keepdims=True)[0]
+    mass = jnp.sum(jnp.exp(lw_all[...] - largest[None]), (0, 1), keepdims=True)[0]
+    out_lw[...] = mine - (largest + jnp.log(mass))
+
+    both_k.wait()
+    both_v.wait()
+    for k in (1, 2, 3):
+        for which in range(2):
+            light_mirror(k, which).wait_recv()
+
+    @pl.when(pos > 0)
+    def _():
+        for q in range(4):
+            for which in range(2):
+                mirror(q, which).wait()
+
+    for i in range(parts):
+        at = tab[1, i]
+        new_k[i, :span, :] = all_k[at]
+        new_v[i, :span, :] = all_v[at]
+
+    @pl.when(pos < 3)
+    def _():
+        for q in range(4):
+            for which in range(2):
+                forward(q, which).wait_send()
+
+    for k in (1, 2, 3):
+        for which in range(2):
+            light(k, which).wait_send()
+            light_mirror(k, which).wait_send()
+    for copy in news:
+        copy.wait_send()
+
+
+def adaptive(
+    activations, norm_gain, w_query, w_key, value_weight, w_output, cache_keys, cache_values,
+    tokens, twisting_table, twist_vec, previous_log_weights, copy_counts,
+):
+    f32, bf16 = jnp.float32, jnp.bfloat16
+    steps, parts, width = activations.shape
+    rows = steps * parts
+    span = cache_keys.shape[1]
+    kvw = w_key.shape[1]
+    qw = w_query.shape[1]
+    groups = kvw // HD
+    pack = steps * (qw // kvw)
+    doms = lax.axis_size("dom")
+    tps = lax.axis_size("tp")
+    middle = HD // 2
+    cap = CAP
+    angles = (span + np.arange(rows) // parts)[:, None] * (
+        500000.0 ** (-2.0 * np.arange(middle) / HD)
+    )
+    cosine = np.concatenate([np.cos(angles)] * 2, 1).astype(np.float32)
+    sine = np.concatenate([-np.sin(angles), np.sin(angles)], 1).astype(np.float32)
+    reward = jnp.sum(twisting_table[tokens].astype(f32), 0)
+    aux = (previous_log_weights + reward).reshape(parts, 1)
+    vmem = pl.BlockSpec(memory_space=pltpu.VMEM)
+    smem = pl.BlockSpec(memory_space=pltpu.SMEM)
+    hbm = pl.BlockSpec(memory_space=pl.ANY)
+    tab = pl.pallas_call(
+        functools.partial(plan_kernel, parts, doms, cap, steps, rows),
+        out_shape=jax.ShapeDtypeStruct((8, HD), jnp.int32),
+        in_specs=[vmem],
+        out_specs=vmem,
+        scratch_shapes=[
+            pltpu.VMEM((doms, 8, HD), f32),
+            pltpu.SemaphoreType.DMA((doms - 1,)),
+            pltpu.SemaphoreType.DMA((doms - 1,)),
+        ],
+        compiler_params=pltpu.CompilerParams(collective_id=5, has_side_effects=True),
+        name="plan",
+    )(copy_counts.reshape(1, parts))
+
+    def hot_branch(hot):
+        result = jax.ShapeDtypeStruct((parts, span + steps, kvw), bf16)
+        dma = pltpu.SemaphoreType.DMA
+        call = pl.pallas_call(
+            functools.partial(main_kernel, steps, parts, doms, tps, cap, hot),
+            out_shape=(
+                jax.ShapeDtypeStruct((rows, width), bf16), result, result,
+                jax.ShapeDtypeStruct((parts, HD), f32),
+            ),
+            in_specs=[hbm, vmem] + [hbm] * 6 + [vmem] * 4 + [smem, vmem],
+            out_specs=(vmem,) * 4,
+            scratch_shapes=[
+                pltpu.VMEM((tps, rows, width), bf16),
+                pltpu.VMEM(w_query.shape, bf16),
+                pltpu.VMEM(w_key.shape, bf16),
+                pltpu.VMEM(value_weight.shape, bf16),
+                pltpu.VMEM(w_output.shape, bf16),
+                pltpu.VMEM((2 * parts, span, kvw), bf16),
+                pltpu.VMEM((2 * parts, span, kvw), bf16),
+                pltpu.VMEM((3 * parts + 3 * cap, span, kvw), bf16),
+                pltpu.VMEM((3 * parts + 3 * cap, span, kvw), bf16),
+                pltpu.VMEM((3, cap // 2, span, kvw), bf16),
+                pltpu.VMEM((3, cap // 2, span, kvw), bf16),
+                pltpu.VMEM((groups, parts, pack, HD), f32),
+                pltpu.VMEM((groups, parts, pack, HD), f32),
+                pltpu.VMEM((groups, parts * pack, span), f32),
+                pltpu.VMEM((rows, qw), bf16),
+                pltpu.VMEM((doms, rows, 2 * kvw), bf16),
+                pltpu.VMEM((tps - 1, rows, width), bf16),
+                pltpu.VMEM((tps - 1, rows, width), bf16),
+                pltpu.VMEM((tps, rows, HD), f32),
+                pltpu.VMEM((doms, parts, HD), f32),
+                dma((9,)),
+                dma((3 * (tps - 1),)), dma((3 * (tps - 1),)),
+                dma((doms - 1,)), dma((doms - 1,)),
+                dma((2,)), dma((2,)),
+                dma((16,)), dma((16,)),
+                dma((12,)), dma((12,)),
+                dma((7,)), dma((7,)),
+            ],
+            compiler_params=pltpu.CompilerParams(
+                collective_id=hot, has_side_effects=True, vmem_limit_bytes=60 << 20
+            ),
+            name=f"main{hot}",
+        )
+
+        def run(act, gain, wq, wk, wv, wo, ck, cv, twist, aux, counts, cosine, sine, tab):
+            attn, new_k, new_v, out_lw = call(
+                act, gain, wq, wk, wv, wo, ck, cv, twist, aux, cosine, sine, tab, tab
+            )
+            return attn, new_k, new_v, out_lw
+
+        return run
+
+    def every(act, gain, wq, wk, wv, wo, ck, cv, twist, aux, counts, cosine, sine, tab):
+        return all_rows(
+            steps, parts, act, gain, wq, wk, wv, wo, ck, cv, twist,
+            jnp.concatenate([aux, counts.astype(f32)], 1), cosine, sine,
+        )
+
+    attn, new_k, new_v, out_lw = lax.switch(
+        tab[4, 0],
+        [hot_branch(hot) for hot in range(4)] + [every],
+        activations.reshape(rows, width), norm_gain.reshape(1, -1), w_query, w_key,
+        value_weight, w_output, cache_keys, cache_values, twist_vec.reshape(1, -1), aux,
+        copy_counts.reshape(parts, 1), jnp.asarray(cosine), jnp.asarray(sine), tab,
+    )
     return attn.reshape(steps, parts, width), new_k, new_v, out_lw[:, 0]
 
 
 def solution(mesh):
-    body = fused if mesh.shape["dom"] == 8 else local
+    body = adaptive if mesh.shape["dom"] == 8 else local
     return jax.shard_map(
         body,
         mesh=mesh,

time: 104 us -> 81.6 us (0.78)
  Pallas kernels: 93.4 us -> 72.6 us
  local copies, waits for them, and re-layouts: 7.38 us -> 5.96 us
    pallas_call x2, Pallas kernels: 93.4 us -> 72.6 us  [the longest x1 64.7 us: run(): call(act, gain, wq, wk, wv, wo, ck, cv, twist, aux, cosine, sine, tab, tab)]
    another operation x3 -> x0, other arithmetic: 1.37 us -> none  [fused(): aux = jnp.stack([previous_log_weights + reward, copy_counts.astype(f32)], 1)]
    unnamed x9 -> x5, local copies, waits for them, and re-layouts: 4.4 us -> 3.18 us
where the time goes in v1:
time: 81.6 us; the launch traced here: 81.9 us
  Pallas kernels  72.6 us (89%)
  local copies, waits for them, and re-layouts  5.96 us (7%)
  other arithmetic  1.42 us (2%)
  between operations  1.31 us (2%)
    pallas_call x1, Pallas kernels, run(): call(act, gain, wq, wk, wv, wo, ck, cv, twist, aux, cosine, sine, tab, tab)  64.7 us
    pallas_call x1, Pallas kernels, adaptive(): pl.pallas_call(functools.partial(plan_kernel, parts, doms, cap, steps, ro...  7.95 us
    unnamed x5, local copies, waits for them, and re-layouts  3.18 us

profile of v1, /device:TPU:0, one launch (start us, length us, event | category | flops | bytes accessed | tf_op | source)
XLA Modules:
  0.0 81.9 jit_solution(10969237623935087297)
XLA Ops:
  0.6 0.0 copy-start
  0.6 0.7 compare_select_fusion
  1.4 0.1 reshape.46
  1.5 0.1 copy-done
  1.6 0.8 gather_fusion
  2.4 0.1 reshape.54
  2.5 0.7 add_bitcast_fusion
  3.2 7.9 %plan.1 = s32[8,128]{1,0:T(8,128)S(1)} custom-call(s32[1,16]{1,0:T(1,128)} %bitcast.26), custom_call_target="tpu_custom_call" | custom-call | tf_op jit(solution)/shard_map/plan/pallas_call | solution.py:989
  11.1 0.5 slice.12
  12.3 65.9 %conditional.1 = (bf16[16,132,256]{2,1,0:T(8,128)(2,1)S(1)}, bf16[16,132,256]{2,1,0:T(8,128)(2,1)S(1)}, bf16[64,1024]{1,0:T(8,128)(2,1)S(1)}, f32[16,128]{1,0:T(8,128)S(1)}) conditional(s32[]{:T(128)} %bitcast.2, (bf16[64,1024]{1,0:T(8,128)(2,1)}, f32[1,4096]{1,0:T(1,128)}, bf16[4096,1024]{1,0:T(8,128)(2,1)}, ...), branch_computations={%region_1.0_spmd, %region_2.0_spmd, %region_3.0_spmd, %region_4.0_... | conditional | flops 48 | bytes 672 | solution.py:1063
  12.3 0.7 copy.36.aux
  13.0 64.7 %main0.1 = (bf16[64,1024]{1,0:T(8,128)(2,1)S(1)}, bf16[16,132,256]{2,1,0:T(8,128)(2,1)S(1)}, bf16[16,132,256]{2,1,0:T(8,128)(2,1)S(1)}, f32[16,128]{1,0:T(8,128)S(1)}) custom-call(bf16[64,1024]{1,0:T(8,128)(2,1)} %get-tuple-element.153.act, f32[1,4096]{1,0:T(1,128)} %get-tuple-element.154.gain, bf16[4096,1024]{1,0:T(8,128)(2,1)} %get-tuple-element.155.wq, ...), custom_call_target="tpu_custom_call" | custom-call | tf_op jit(solution)/shard_map/cond/branch_0_fun/main0/pallas_call | solution.py:1050
  78.2 0.6 slice_reduce_fusion
  78.9 1.2 %copy.40 = bf16[16,132,256]{2,0,1:T(8,128)(2,1)} copy(bf16[16,132,256]{2,1,0:T(8,128)(2,1)S(1)} %get-tuple-element.445) | data formatting | bytes 2162688
  80.1 1.2 %copy.41 = bf16[16,132,256]{2,0,1:T(8,128)(2,1)} copy(bf16[16,132,256]{2,1,0:T(8,128)(2,1)S(1)} %get-tuple-element.446) | data formatting | bytes 2162688
  81.2 0.7 copy.63
  (2 shorter events, 0.0 us)
Async XLA Ops:
  0.6 1.0 %copy-start = (bf16[128256]{0:T(1024)(128)(2,1)S(1)}, bf16[128256]{0:T(1024)(128)(2,1)}, u32[]{:S(2)}) copy-start(bf16[128256]{0:T(1024)(128)(2,1)} %param.29) | copy-start | bytes 769540

commit v2 on v1

--- a/solution.py
+++ b/solution.py
@@ -10,7 +10,8 @@
 
 D = 4096
 HD = 128
-CAP = 8
+CAP = 6
+HOT_CAP = 4
 
 
 def rotate(tensor, positions):
@@ -495,7 +496,7 @@
             pltpu.SemaphoreType.DMA((32,)),
         ],
         compiler_params=pltpu.CompilerParams(
-            collective_id=4, has_side_effects=True, vmem_limit_bytes=56 << 20
+            collective_id=4, has_side_effects=True, vmem_limit_bytes=52 << 20
         ),
         name="layer",
     )(act, gain, wq, wk, wv, wo, ck, cv, twist, aux, cosine, sine)
@@ -506,12 +507,16 @@
         in_specs=[pl.BlockSpec(memory_space=pltpu.SMEM), vmem, hbm, hbm],
         out_specs=(vmem, vmem),
         scratch_shapes=[pltpu.SemaphoreType.DMA((2 * parts,))],
+        compiler_params=pltpu.CompilerParams(vmem_limit_bytes=8 << 20),
         name="select",
     )(anc, fresh_sel, all_k, all_v)
     return attn, new_k, new_v, out_lw
 
 
-def plan_kernel(parts, doms, cap, steps, rows, cnt, tab, cnt_all, send, recv):
+def plan_kernel(
+    parts, doms, cap, hot_cap, steps, rows,
+    cnt, ck, cv, tab, chip_k, chip_v, cnt_all, send, recv, loc, sib_send, sib_recv,
+):
     f32, bf16, i32 = jnp.float32, jnp.bfloat16, jnp.int32
     me_d = lax.axis_index("dom")
     me_t = lax.axis_index("tp")
@@ -524,6 +529,11 @@
         pl.semaphore_signal(
             barrier, inc=1, device_id=((me_d + k) % doms, me_t), device_id_type=MESH
         )
+    owns = []
+    for i, (src, dst) in enumerate(((ck, chip_k), (cv, chip_v))):
+        copy = pltpu.make_async_copy(src, dst.at[pl.ds(0, parts)], loc.at[i])
+        copy.start()
+        owns.append(copy)
     cnt_all[me_d] = jnp.zeros(cnt_all.shape[1:], f32)
     cnt_all[me_d, :, :parts] = jnp.broadcast_to(cnt[...].astype(f32), (8, parts))
     pl.semaphore_wait(barrier, doms - 1)
@@ -536,6 +546,15 @@
         )
         copy.start()
         copies.append(copy)
+    swaps = []
+    for i, (src, dst) in enumerate(((ck, chip_k), (cv, chip_v))):
+        copy = pltpu.make_async_remote_copy(
+            src_ref=src, dst_ref=dst.at[pl.ds(parts, parts)],
+            send_sem=sib_send.at[i], recv_sem=sib_recv.at[i],
+            device_id=(me_d + 1 - 2 * core, me_t), device_id_type=MESH,
+        )
+        copy.start()
+        swaps.append(copy)
     for copy in copies:
         copy.wait()
     whole = parts * doms
@@ -586,14 +605,20 @@
     place_here = places[:, HD : 2 * HD]
     place_any = places[:, 2 * HD :]
     local_row = j % parts + parts * (owner % 2 + core - 2 * core * (owner % 2))
-    picked = need_send & (place_send == lane % cap) & (home == chip)
+    half = cap // 2
+    entry = lane % cap
+    picked = need_send & (place_send == 2 * (entry % half) + entry // half) & (home == chip)
     sources = jnp.sum(jnp.where(picked, local_row, 0).astype(f32), 0, keepdims=True)
     hx, hy = home % 2, home // 2
     away = (hx + x - 2 * x * hx) + 2 * (hy + y - 2 * y * hy)
     value = jnp.where(
         away == 0,
         local_row,
-        jnp.where(light, 3 * parts + (away - 1) * cap + place_here, 2 * parts + j % parts),
+        jnp.where(
+            light,
+            3 * parts + (away - 1) * cap + place_here % 2 * half + place_here // 2,
+            2 * parts + j % parts,
+        ),
     )
     rank = lane * doms + me_d
     mine = (starts <= rank) & (rank < ends)
@@ -603,26 +628,30 @@
     row = lax.broadcasted_iota(i32, (1, HD), 1)
     target = (old // parts) * rows + (row % 8) * parts + old % parts
     target = jnp.where(row % 8 < steps, target, -1)
-    longest = jnp.max(
-        jnp.where(need_any, place_any + 1, 0).astype(f32), (0, 1), keepdims=True
+    room = jnp.where(home == heavy // 2, hot_cap, cap)
+    over = jnp.max(
+        (need_any & (place_any >= room)).astype(f32), (0, 1), keepdims=True
     ).astype(i32)
     base = parts * (heavy % 2 + core - 2 * core * (heavy % 2))
-    branch = jnp.where(longest <= cap, heavy // 2, 4)
+    branch = jnp.where(over == 0, heavy // 2, 4)
     tab[0:1, :] = sources.astype(i32)
     tab[1:2, :] = index.astype(i32)
     tab[2:3, :] = jnp.broadcast_to(base, (1, HD))
     tab[3:4, :] = target
     tab[4:5, :] = jnp.broadcast_to(branch, (1, HD))
     tab[5:8, :] = jnp.zeros((3, HD), i32)
+    for copy in owns + swaps:
+        copy.wait()
 
 
 def main_kernel(
-    steps, parts, doms, tps, cap, hot,
-    act, gain, wq, wk, wv, wo, ck, cv, twist, aux, cosine, sine, tab, tabv,
+    steps, parts, doms, tps, cap, hot_cap, hot,
+    act, gain, wq, wk, wv, wo, chip_k, chip_v, twist, tokens, table, prev, cosine, sine,
+    tab, tabv,
     attn_out, new_k, new_v, out_lw,
-    act_all, wq_v, wk_v, wv_v, wo_v, chip_k, chip_v, all_k, all_v, send_k, send_v,
+    act_all, wq_v, wk_v, wv_v, wo_v, all_k, all_v, send_k, send_v,
     qs, cx, sc1, ctx_b, fresh_all, rs_send, rs_recv, sc_all, lw_all,
-    loc, tp_send, tp_recv, lw_send, lw_recv, sib_send, sib_recv,
+    loc, tp_send, tp_recv, lw_send, lw_recv,
     hv_send, hv_recv, li_send, li_recv, fr_send, fr_recv,
 ):
     f32, bf16 = jnp.float32, jnp.bfloat16
@@ -633,7 +662,7 @@
     groups = kvw // HD
     per = wq.shape[1] // kvw
     pack = steps * per
-    span = ck.shape[1]
+    span = chip_k.shape[1]
     c = me_d % 2
     x = (me_d // 2) % 2
     y = me_d // 4
@@ -663,8 +692,6 @@
         return copy
 
     own_act = fetch(0, act, act_all.at[me_t])
-    load_ck = fetch(4, ck, chip_k.at[pl.ds(0, parts)])
-    load_cv = fetch(5, cv, chip_v.at[pl.ds(0, parts)])
     load_k = fetch(2, wk, wk_v)
     load_v = fetch(3, wv, wv_v)
     load_q = fetch(1, wq, wq_v)
@@ -686,13 +713,9 @@
         return copy
 
     acts = [tp_push(0, k, act, act_all.at[me_t]) for k in range(1, tps)]
-    swaps = []
-    for i, (src, dst) in enumerate(((ck, chip_k), (cv, chip_v))):
-        copy = push(src, dst.at[pl.ds(parts, parts)], sib_send.at[i], sib_recv.at[i], sib, me_t)
-        copy.start()
-        swaps.append(copy)
-
     lane_rows = cap // 2
+    hot_lane = hot_cap // 2
+    rel = rx + 2 * ry
     hot_rows = parts // 2
     chunk = hot_rows // 4
 
@@ -708,25 +731,49 @@
     def mirror(q, which):
         return hot_copy(q, which, sib, 8)
 
-    def light_area(ref, k):
-        return ref.at[pl.ds(3 * parts + (k - 1) * cap + lane_rows * c, lane_rows)]
-
-    def light(k, which):
-        i = (k - 1) * 2 + which
+    def light_part(ref, base, piece):
+        if piece == 0:
+            return ref.at[pl.ds(base, hot_lane)]
+        return ref.at[pl.ds(base + hot_lane, lane_rows - hot_lane)]
+
+    def light_area(which, k, piece):
+        base = 3 * parts + (k - 1) * cap + lane_rows * c
+        return light_part((all_k, all_v)[which], base, piece)
+
+    def light(k, which, piece):
+        i = ((k - 1) * 2 + which) * 2 + piece
         return push(
-            (send_k, send_v)[which].at[k - 1], light_area((all_k, all_v)[which], k),
+            light_part((send_k, send_v)[which].at[k - 1], 0, piece),
+            light_area(which, k, piece),
             li_send.at[i], li_recv.at[i], (xn, yn, dn)[k - 1], me_t,
         )
 
-    def light_mirror(k, which):
-        i = 6 + (k - 1) * 2 + which
-        area = light_area((all_k, all_v)[which], k)
+    def light_mirror(k, which, piece):
+        i = 12 + ((k - 1) * 2 + which) * 2 + piece
+        area = light_area(which, k, piece)
         return push(area, area, li_send.at[i], li_recv.at[i], sib, me_t)
 
-    load_ck.wait()
-    load_cv.wait()
-    for copy in swaps:
-        copy.wait()
+    def send_lights(count, pieces):
+        for k in (3, 1, 2):
+            for t in range(count):
+                at = tab[0, k * cap + lane_rows * c + t]
+                send_k[k - 1, t] = chip_k[at]
+                send_v[k - 1, t] = chip_v[at]
+            for piece in range(pieces):
+                for which in range(2):
+                    light(k, which, piece).start()
+
+    def arrived(k):
+        for which in range(2):
+            light(k, which, 0).wait_recv()
+            light_mirror(k, which, 0).start()
+
+        @pl.when(rel != k)
+        def _():
+            for which in range(2):
+                light(k, which, 1).wait_recv()
+                light_mirror(k, which, 1).start()
+
     both_k = fetch(7, chip_k, all_k.at[pl.ds(0, 2 * parts)])
     both_v = fetch(8, chip_v, all_v.at[pl.ds(0, 2 * parts)])
 
@@ -740,13 +787,9 @@
                 for which in range(2):
                     forward(i // chunk, which).start()
 
-    for k in (3, 1, 2):
-        for t in range(lane_rows):
-            at = tab[0, k * cap + lane_rows * c + t]
-            send_k[k - 1, t] = chip_k[at]
-            send_v[k - 1, t] = chip_v[at]
-        for which in range(2):
-            light(k, which).start()
+    @pl.when(pos > 0)
+    def _():
+        send_lights(lane_rows, 2)
 
     def relay(*list_of):
         for where, q in list_of:
@@ -759,6 +802,9 @@
                         forward(q, which).start()
                     mirror(q, which).start()
 
+    relay((1, 0))
+    relay((1, 1))
+    relay((1, 2))
     own_act.wait()
     for copy in acts:
         copy.wait()
@@ -808,7 +854,11 @@
         turned = turn(query[:, h * HD : (h + 1) * HD])
         for s in range(steps):
             qs[g, :, s * per + j, :] = turned[s * parts : (s + 1) * parts]
-    relay((1, 0))
+    relay((1, 3), (2, 0))
+
+    @pl.when(pos == 0)
+    def _():
+        send_lights(hot_lane, 1)
 
     lines = parts * pack
     row = lax.broadcasted_iota(jnp.int32, (lines, rows), 0)
@@ -844,15 +894,12 @@
             cx[g, n] = extra[part] + jnp.dot(
                 far[part], chip_v[n, :, lanes], preferred_element_type=f32
             )
-        if g == 0:
-            relay((1, 1), (2, 0))
     for h in range(groups * per):
         g, j = h // per, h % per
         for s in range(steps):
             ctx_b[s * parts : (s + 1) * parts, h * HD : (h + 1) * HD] = cx[
                 g, :, s * per + j, :
             ].astype(bf16)
-    relay((1, 2), (2, 1), (3, 0))
     load_o.wait()
 
     def mix(p):
@@ -866,7 +913,12 @@
         rs_send[k - 1] = mix((me_t + k) % tps).astype(bf16)
         sums.append(tp_push(tps - 1, k, rs_send.at[k - 1], rs_recv.at[k - 1]))
     head = mix(me_t)
-    relay((1, 3), (2, 2), (3, 1))
+    relay((2, 1))
+    relay((2, 2))
+    relay((2, 3), (3, 0))
+    relay((3, 1))
+    arrived(1)
+    arrived(2)
     for copy in news:
         copy.wait_recv()
     passed = [fresh_copy(4 + i, b + c, sib) for i, b in enumerate((dn - c, xn - c, yn - c))]
@@ -885,7 +937,8 @@
     scores = [
         tp_push(2 * (tps - 1), k, sc_all.at[me_t], sc_all.at[me_t]) for k in range(1, tps)
     ]
-    relay((2, 3), (3, 2))
+    relay((3, 2))
+    arrived(3)
     for copy in scores:
         copy.wait()
     both = sc_all[0]
@@ -895,7 +948,24 @@
     total = score[:parts]
     for s in range(1, steps):
         total = total + score[s * parts : (s + 1) * parts]
-    mine = jnp.broadcast_to(aux[...] + total, (parts, HD))
+    count = table.shape[0]
+    deep = lax.broadcasted_iota(jnp.int32, (rows, parts), 0) % parts
+    broad = lax.broadcasted_iota(jnp.int32, (rows, parts), 1)
+    names = jnp.concatenate(
+        [jnp.broadcast_to(tokens[s : s + 1, :], (parts, parts)) for s in range(steps)], 0
+    )
+    name = jnp.sum(jnp.where(deep == broad, names, 0).astype(f32), -1, keepdims=True)
+    name = name.astype(jnp.int32)
+    line = lax.broadcasted_iota(jnp.int32, (rows, count), 1)
+    found = jnp.dot(
+        (line == name // HD).astype(f32).astype(bf16), table[...], preferred_element_type=f32
+    )
+    gift = jnp.sum(jnp.where(lane == name % HD, found, 0.0), -1, keepdims=True)
+    for s in range(steps):
+        total = total + gift[s * parts : (s + 1) * parts]
+    past = jnp.where(deep[:parts] == broad[:parts], prev[...], 0.0)
+    total = total + jnp.sum(past, -1, keepdims=True)
+    mine = jnp.broadcast_to(total, (parts, HD))
     lw_all[me_d] = mine
     lws = []
     for k in range(1, doms):
@@ -906,10 +976,6 @@
         copy.start()
         lws.append(copy)
 
-    for k in (1, 2, 3):
-        for which in range(2):
-            light(k, which).wait_recv()
-            light_mirror(k, which).start()
     relay((3, 3))
     for copy in passed:
         copy.wait()
@@ -933,7 +999,12 @@
     both_v.wait()
     for k in (1, 2, 3):
         for which in range(2):
-            light_mirror(k, which).wait_recv()
+            light_mirror(k, which, 0).wait()
+
+        @pl.when(rel != k)
+        def _():
+            for which in range(2):
+                light_mirror(k, which, 1).wait()
 
     @pl.when(pos > 0)
     def _():
@@ -954,8 +1025,14 @@
 
     for k in (1, 2, 3):
         for which in range(2):
-            light(k, which).wait_send()
-            light_mirror(k, which).wait_send()
+            light(k, which, 0).wait_send()
+
+    @pl.when(pos > 0)
+    def _():
+        for k in (1, 2, 3):
+            for which in range(2):
+                light(k, which, 1).wait_send()
+
     for copy in news:
         copy.wait_send()
 
@@ -981,35 +1058,35 @@
     )
     cosine = np.concatenate([np.cos(angles)] * 2, 1).astype(np.float32)
     sine = np.concatenate([-np.sin(angles), np.sin(angles)], 1).astype(np.float32)
-    reward = jnp.sum(twisting_table[tokens].astype(f32), 0)
-    aux = (previous_log_weights + reward).reshape(parts, 1)
     vmem = pl.BlockSpec(memory_space=pltpu.VMEM)
     smem = pl.BlockSpec(memory_space=pltpu.SMEM)
     hbm = pl.BlockSpec(memory_space=pl.ANY)
-    tab = pl.pallas_call(
-        functools.partial(plan_kernel, parts, doms, cap, steps, rows),
-        out_shape=jax.ShapeDtypeStruct((8, HD), jnp.int32),
-        in_specs=[vmem],
-        out_specs=vmem,
+    dma = pltpu.SemaphoreType.DMA
+    both = jax.ShapeDtypeStruct((2 * parts, span, kvw), bf16)
+    tab, chip_k, chip_v = pl.pallas_call(
+        functools.partial(plan_kernel, parts, doms, cap, HOT_CAP, steps, rows),
+        out_shape=(jax.ShapeDtypeStruct((8, HD), jnp.int32), both, both),
+        in_specs=[vmem, hbm, hbm],
+        out_specs=(vmem,) * 3,
         scratch_shapes=[
             pltpu.VMEM((doms, 8, HD), f32),
-            pltpu.SemaphoreType.DMA((doms - 1,)),
-            pltpu.SemaphoreType.DMA((doms - 1,)),
+            dma((doms - 1,)), dma((doms - 1,)), dma((2,)), dma((2,)), dma((2,)),
         ],
-        compiler_params=pltpu.CompilerParams(collective_id=5, has_side_effects=True),
+        compiler_params=pltpu.CompilerParams(
+            collective_id=5, has_side_effects=True, vmem_limit_bytes=16 << 20
+        ),
         name="plan",
-    )(copy_counts.reshape(1, parts))
+    )(copy_counts.reshape(1, parts), cache_keys, cache_values)
 
     def hot_branch(hot):
         result = jax.ShapeDtypeStruct((parts, span + steps, kvw), bf16)
-        dma = pltpu.SemaphoreType.DMA
         call = pl.pallas_call(
-            functools.partial(main_kernel, steps, parts, doms, tps, cap, hot),
+            functools.partial(main_kernel, steps, parts, doms, tps, cap, HOT_CAP, hot),
             out_shape=(
                 jax.ShapeDtypeStruct((rows, width), bf16), result, result,
                 jax.ShapeDtypeStruct((parts, HD), f32),
             ),
-            in_specs=[hbm, vmem] + [hbm] * 6 + [vmem] * 4 + [smem, vmem],
+            in_specs=[hbm, vmem] + [hbm] * 4 + [vmem] * 8 + [smem, vmem],
             out_specs=(vmem,) * 4,
             scratch_shapes=[
                 pltpu.VMEM((tps, rows, width), bf16),
@@ -1017,8 +1094,6 @@
                 pltpu.VMEM(w_key.shape, bf16),
                 pltpu.VMEM(value_weight.shape, bf16),
                 pltpu.VMEM(w_output.shape, bf16),
-                pltpu.VMEM((2 * parts, span, kvw), bf16),
-                pltpu.VMEM((2 * parts, span, kvw), bf16),
                 pltpu.VMEM((3 * parts + 3 * cap, span, kvw), bf16),
                 pltpu.VMEM((3 * parts + 3 * cap, span, kvw), bf16),
                 pltpu.VMEM((3, cap // 2, span, kvw), bf16),
@@ -1035,37 +1110,44 @@
                 dma((9,)),
                 dma((3 * (tps - 1),)), dma((3 * (tps - 1),)),
                 dma((doms - 1,)), dma((doms - 1,)),
-                dma((2,)), dma((2,)),
                 dma((16,)), dma((16,)),
-                dma((12,)), dma((12,)),
+                dma((24,)), dma((24,)),
                 dma((7,)), dma((7,)),
             ],
             compiler_params=pltpu.CompilerParams(
-                collective_id=hot, has_side_effects=True, vmem_limit_bytes=60 << 20
+                collective_id=hot, has_side_effects=True, vmem_limit_bytes=42 << 20
             ),
             name=f"main{hot}",
         )
 
-        def run(act, gain, wq, wk, wv, wo, ck, cv, twist, aux, counts, cosine, sine, tab):
-            attn, new_k, new_v, out_lw = call(
-                act, gain, wq, wk, wv, wo, ck, cv, twist, aux, cosine, sine, tab, tab
+        def run(
+            act, gain, wq, wk, wv, wo, chip_k, chip_v, twist, tokens, table, prev, cosine,
+            sine, tab, ck, cv, counts,
+        ):
+            return call(
+                act, gain, wq, wk, wv, wo, chip_k, chip_v, twist, tokens, table, prev,
+                cosine, sine, tab, tab,
             )
-            return attn, new_k, new_v, out_lw
 
         return run
 
-    def every(act, gain, wq, wk, wv, wo, ck, cv, twist, aux, counts, cosine, sine, tab):
+    def every(
+        act, gain, wq, wk, wv, wo, chip_k, chip_v, twist, tokens, table, prev, cosine,
+        sine, tab, ck, cv, counts,
+    ):
+        reward = jnp.sum(table.reshape(-1)[tokens].astype(f32), 0)
+        aux = jnp.stack([prev[0] + reward, counts.astype(f32)], 1)
         return all_rows(
-            steps, parts, act, gain, wq, wk, wv, wo, ck, cv, twist,
-            jnp.concatenate([aux, counts.astype(f32)], 1), cosine, sine,
+            steps, parts, act, gain, wq, wk, wv, wo, ck, cv, twist, aux, cosine, sine
         )
 
     attn, new_k, new_v, out_lw = lax.switch(
         tab[4, 0],
         [hot_branch(hot) for hot in range(4)] + [every],
         activations.reshape(rows, width), norm_gain.reshape(1, -1), w_query, w_key,
-        value_weight, w_output, cache_keys, cache_values, twist_vec.reshape(1, -1), aux,
-        copy_counts.reshape(parts, 1), jnp.asarray(cosine), jnp.asarray(sine), tab,
+        value_weight, w_output, chip_k, chip_v, twist_vec.reshape(1, -1), tokens,
+        twisting_table.reshape(-1, HD), previous_log_weights.reshape(1, parts),
+        jnp.asarray(cosine), jnp.asarray(sine), tab, cache_keys, cache_values, copy_counts,
     )
     return attn.reshape(steps, parts, width), new_k, new_v, out_lw[:, 0]
 

time: 81.6 us -> 65.1 us (0.80)
  Pallas kernels: 72.6 us -> 58.5 us
  local copies, waits for them, and re-layouts: 5.96 us -> 4.2 us
  other arithmetic: 1.42 us -> 0 us
    pallas_call x2, Pallas kernels: 72.6 us -> 58.5 us  [the longest x1 49.6 us: run(): call(act, gain, wq, wk, wv, wo, chip_k, chip_v, twist, tokens, table, pre...]
    unnamed x5 -> x13, local copies, waits for them, and re-layouts: 3.18 us -> 3.06 us
where the time goes in v2:
time: 65.1 us; the launch traced here: 64.7 us
  Pallas kernels  58.5 us (90%)
  local copies, waits for them, and re-layouts  4.2 us (6%)
  between operations  1.38 us (2%)
    pallas_call x1, Pallas kernels, run(): call(act, gain, wq, wk, wv, wo, chip_k, chip_v, twist, tokens, table, pre...  49.6 us
    pallas_call x1, Pallas kernels, adaptive(): pl.pallas_call(functools.partial(plan_kernel, parts, doms, cap, HOT_CAP,...  8.92 us
    unnamed x13, local copies, waits for them, and re-layouts  3.06 us

profile of v2, /device:TPU:0, one launch (start us, length us, event | category | flops | bytes accessed | tf_op | source)
XLA Modules:
  0.0 64.7 jit_solution(5285466062184699292)
XLA Ops:
  0.6 0.0 copy-start.8
  0.6 0.0 copy-start.7
  0.7 0.0 copy-start.2
  0.7 0.0 copy-start.6
  0.7 0.0 copy-start.5
  0.7 8.9 %plan.1 = (s32[8,128]{1,0:T(8,128)S(1)}, bf16[32,128,256]{2,1,0:T(8,128)(2,1)S(1)}, bf16[32,128,256]{2,1,0:T(8,128)(2,1)S(1)}) custom-call(s32[1,16]{1,0:T(1,128)} %bitcast.42, bf16[16,128,256]{2,1,0:T(8,128)(2,1)} %ck.1, bf16[16,128,256]{2,1,0:T(8,128)(2,1)} %cv.1), custom_call_target="tpu_custom_call" | custom-call | tf_op jit(solution)/shard_map/plan/pallas_call | solution.py:1066
  9.6 0.5 slice.12
  10.8 0.0 copy-done.8
  10.8 0.0 copy-done.7
  10.8 0.0 copy-done.2
  10.8 0.0 copy-done.6
  10.8 0.0 copy-done.5
  10.8 50.2 %conditional.1 = (bf16[16,132,256]{2,1,0:T(8,128)(2,1)S(1)}, bf16[16,132,256]{2,1,0:T(8,128)(2,1)S(1)}, bf16[64,1024]{1,0:T(8,128)(2,1)S(1)}, f32[16,128]{1,0:T(8,128)S(1)}) conditional(s32[]{:T(128)} %bitcast.11, (bf16[128256]{0:T(1024)(128)(2,1)}, f32[16]{0:T(128)S(1)}, bf16[64,1024]{1,0:T(8,128)(2,1)}, ...), branch_computations={%region_0.0_spmd, %region_1.0_spmd, %region_2.0_spmd, %region_3.0_... | conditional | flops 1328 | bytes 71441808 | solution.py:1144
  10.9 49.6 %main1.1 = (bf16[64,1024]{1,0:T(8,128)(2,1)S(1)}, bf16[16,132,256]{2,1,0:T(8,128)(2,1)S(1)}, bf16[16,132,256]{2,1,0:T(8,128)(2,1)S(1)}, f32[16,128]{1,0:T(8,128)S(1)}) custom-call(bf16[64,1024]{1,0:T(8,128)(2,1)} %get-tuple-element.199.act, f32[1,4096]{1,0:T(1,128)S(1)} %get-tuple-element.200.gain, bf16[4096,1024]{1,0:T(8,128)(2,1)} %get-tuple-element.201.wq, ...), custom_call_target="tpu_custom_call" | custom-call | tf_op jit(solution)/shard_map/cond/branch_1_fun/main1/pallas_call | solution.py:1127
  61.0 0.6 slice_reduce_fusion
  61.6 1.2 %copy.28 = bf16[16,132,256]{2,0,1:T(8,128)(2,1)} copy(bf16[16,132,256]{2,1,0:T(8,128)(2,1)S(1)} %get-tuple-element.306) | data formatting | bytes 2162688
  62.8 1.2 %copy.29 = bf16[16,132,256]{2,0,1:T(8,128)(2,1)} copy(bf16[16,132,256]{2,1,0:T(8,128)(2,1)S(1)} %get-tuple-element.307) | data formatting | bytes 2162688
  64.0 0.7 %copy.51 = bf16[4,16,1024]{2,1,0:T(8,128)(2,1)} copy(bf16[4,16,1024]{2,1,0:T(8,128)(2,1)S(1)} %bitcast.32) | data formatting | bytes 262144
Async XLA Ops:
  0.6 10.2 %copy-start.8 = (s32[16]{0:T(128)S(1)}, s32[16]{0:T(128)}, u32[]{:S(2)}) copy-start(s32[16]{0:T(128)} %param.32) | copy-start | bytes 196
  0.6 10.2 %copy-start.7 = (f32[16]{0:T(128)S(1)}, f32[16]{0:T(128)}, u32[]{:S(2)}) copy-start(f32[16]{0:T(128)} %param.31) | copy-start | bytes 196
  0.7 10.2 %copy-start.2 = (bf16[4096,256]{1,0:T(8,128)(2,1)S(1)}, bf16[4096,256]{1,0:T(8,128)(2,1)}, u32[]{:S(2)}) copy-start(bf16[4096,256]{1,0:T(8,128)(2,1)} %param.23) | copy-start | bytes 6291460
  0.7 10.2 %copy-start.6 = (f32[1024]{0:T(1024)S(1)}, f32[1024]{0:T(1024)}, u32[]{:S(2)}) copy-start(f32[1024]{0:T(1024)} %param.30) | copy-start | bytes 12292
  0.7 10.2 %copy-start.5 = (f32[4096]{0:T(1024)S(1)}, f32[4096]{0:T(1024)}, u32[]{:S(2)}) copy-start(f32[4096]{0:T(1024)} %param.21) | copy-start | bytes 49156

commit v3 on v2

--- a/solution.py
+++ b/solution.py
@@ -12,6 +12,7 @@
 HD = 128
 CAP = 6
 HOT_CAP = 4
+EARLY = 1
 
 
 def rotate(tensor, positions):
@@ -514,8 +515,9 @@
 
 
 def plan_kernel(
-    parts, doms, cap, hot_cap, steps, rows,
-    cnt, ck, cv, tab, chip_k, chip_v, cnt_all, send, recv, loc, sib_send, sib_recv,
+    parts, doms, tps, cap, hot_cap, steps, rows,
+    cnt, act, ck, cv, tab, chip_k, chip_v, act_part,
+    cnt_all, send, recv, loc, sib_send, sib_recv, tp_send, tp_recv,
 ):
     f32, bf16, i32 = jnp.float32, jnp.bfloat16, jnp.int32
     me_d = lax.axis_index("dom")
@@ -525,6 +527,10 @@
     y = me_d // 4
     chip = me_d // 2
     barrier = pltpu.get_barrier_semaphore()
+    for k in range(1, tps):
+        pl.semaphore_signal(
+            barrier, inc=1, device_id=(me_d, (me_t + k) % tps), device_id_type=MESH
+        )
     for k in range(1, doms):
         pl.semaphore_signal(
             barrier, inc=1, device_id=((me_d + k) % doms, me_t), device_id_type=MESH
@@ -534,9 +540,13 @@
         copy = pltpu.make_async_copy(src, dst.at[pl.ds(0, parts)], loc.at[i])
         copy.start()
         owns.append(copy)
+    early = act.at[pl.ds(0, act_part.shape[1])]
+    copy = pltpu.make_async_copy(early, act_part.at[me_t], loc.at[2])
+    copy.start()
+    owns.append(copy)
     cnt_all[me_d] = jnp.zeros(cnt_all.shape[1:], f32)
     cnt_all[me_d, :, :parts] = jnp.broadcast_to(cnt[...].astype(f32), (8, parts))
-    pl.semaphore_wait(barrier, doms - 1)
+    pl.semaphore_wait(barrier, tps + doms - 2)
     copies = []
     for k in range(1, doms):
         copy = pltpu.make_async_remote_copy(
@@ -547,6 +557,14 @@
         copy.start()
         copies.append(copy)
     swaps = []
+    for k in range(1, tps):
+        copy = pltpu.make_async_remote_copy(
+            src_ref=early, dst_ref=act_part.at[me_t],
+            send_sem=tp_send.at[k - 1], recv_sem=tp_recv.at[k - 1],
+            device_id=(me_d, (me_t + k) % tps), device_id_type=MESH,
+        )
+        copy.start()
+        swaps.append(copy)
     for i, (src, dst) in enumerate(((ck, chip_k), (cv, chip_v))):
         copy = pltpu.make_async_remote_copy(
             src_ref=src, dst_ref=dst.at[pl.ds(parts, parts)],
@@ -646,8 +664,8 @@
 
 def main_kernel(
     steps, parts, doms, tps, cap, hot_cap, hot,
-    act, gain, wq, wk, wv, wo, chip_k, chip_v, twist, tokens, table, prev, cosine, sine,
-    tab, tabv,
+    act, act_part, gain, wq, wk, wv, wo, chip_k, chip_v, twist, tokens, table, prev,
+    cosine, sine, tab, tabv,
     attn_out, new_k, new_v, out_lw,
     act_all, wq_v, wk_v, wv_v, wo_v, all_k, all_v, send_k, send_v,
     qs, cx, sc1, ctx_b, fresh_all, rs_send, rs_recv, sc_all, lw_all,
@@ -691,7 +709,9 @@
         copy.start()
         return copy
 
-    own_act = fetch(0, act, act_all.at[me_t])
+    first = act_part.shape[1]
+    later = act.at[pl.ds(first, rows - first)]
+    own_act = fetch(0, later, act_all.at[me_t])
     load_k = fetch(2, wk, wk_v)
     load_v = fetch(3, wv, wv_v)
     load_q = fetch(1, wq, wq_v)
@@ -712,7 +732,7 @@
         copy.start()
         return copy
 
-    acts = [tp_push(0, k, act, act_all.at[me_t]) for k in range(1, tps)]
+    acts = [tp_push(0, k, later, act_all.at[me_t]) for k in range(1, tps)]
     lane_rows = cap // 2
     hot_lane = hot_cap // 2
     rel = rx + 2 * ry
@@ -753,15 +773,13 @@
         area = light_area(which, k, piece)
         return push(area, area, li_send.at[i], li_recv.at[i], sib, me_t)
 
-    def send_lights(count, pieces):
-        for k in (3, 1, 2):
-            for t in range(count):
-                at = tab[0, k * cap + lane_rows * c + t]
-                send_k[k - 1, t] = chip_k[at]
-                send_v[k - 1, t] = chip_v[at]
-            for piece in range(pieces):
-                for which in range(2):
-                    light(k, which, piece).start()
+    def send_lights(when, kinds, pieces):
+        @pl.when(when)
+        def _():
+            for k in kinds:
+                for piece in range(pieces):
+                    for which in range(2):
+                        light(k, which, piece).start()
 
     def arrived(k):
         for which in range(2):
@@ -773,9 +791,6 @@
             for which in range(2):
                 light(k, which, 1).wait_recv()
                 light_mirror(k, which, 1).start()
-
-    both_k = fetch(7, chip_k, all_k.at[pl.ds(0, 2 * parts)])
-    both_v = fetch(8, chip_v, all_v.at[pl.ds(0, 2 * parts)])
 
     @pl.when(pos == 0)
     def _():
@@ -787,9 +802,20 @@
                 for which in range(2):
                     forward(i // chunk, which).start()
 
-    @pl.when(pos > 0)
-    def _():
-        send_lights(lane_rows, 2)
+    for k in (2, 1, 3):
+        for t in range(lane_rows):
+            at = tab[0, k * cap + lane_rows * c + t]
+            send_k[k - 1, t] = chip_k[at]
+            send_v[k - 1, t] = chip_v[at]
+    send_lights((pos == 1) & (rel == 1), (1,), 2)
+    send_lights((pos == 1) & (rel == 2), (2,), 2)
+    send_lights((pos == 3) & (rel == 1), (2, 1), 2)
+    send_lights((pos == 3) & (rel == 2), (1, 2), 2)
+    send_lights(pos == 2, (3, 2, 1), 2)
+    send_lights((pos == 0) & (c == 0), (3, 1), 1)
+    send_lights((pos == 0) & (c == 1), (2,), 1)
+    both_k = fetch(7, chip_k, all_k.at[pl.ds(0, 2 * parts)])
+    both_v = fetch(8, chip_v, all_v.at[pl.ds(0, 2 * parts)])
 
     def relay(*list_of):
         for where, q in list_of:
@@ -804,18 +830,21 @@
 
     relay((1, 0))
     relay((1, 1))
-    relay((1, 2))
     own_act.wait()
     for copy in acts:
         copy.wait()
+
+    def features(t):
+        return jnp.concatenate([act_part[t], act_all[t]], 0).astype(f32)
+
     square = jnp.zeros((rows, 1), f32)
     for t in range(tps):
-        u = act_all[t].astype(f32)
+        u = features(t)
         square = square + jnp.sum(u * u, -1, keepdims=True)
     inv = lax.rsqrt(square / (width * tps) + 1e-05)
     normed = []
     for t in range(tps):
-        u = act_all[t].astype(f32)
+        u = features(t)
         normed.append((u * inv * gain[:, t * width : (t + 1) * width]).astype(bf16))
 
     def project(w):
@@ -854,11 +883,7 @@
         turned = turn(query[:, h * HD : (h + 1) * HD])
         for s in range(steps):
             qs[g, :, s * per + j, :] = turned[s * parts : (s + 1) * parts]
-    relay((1, 3), (2, 0))
-
-    @pl.when(pos == 0)
-    def _():
-        send_lights(hot_lane, 1)
+    relay((1, 2), (2, 0))
 
     lines = parts * pack
     row = lax.broadcasted_iota(jnp.int32, (lines, rows), 0)
@@ -913,23 +938,20 @@
         rs_send[k - 1] = mix((me_t + k) % tps).astype(bf16)
         sums.append(tp_push(tps - 1, k, rs_send.at[k - 1], rs_recv.at[k - 1]))
     head = mix(me_t)
-    relay((2, 1))
+    relay((1, 3), (2, 1))
+    send_lights((pos == 0) & (c == 0), (2,), 1)
+    send_lights((pos == 0) & (c == 1), (3, 1), 1)
+    send_lights((pos == 1) & (rel == 1), (2, 3), 2)
+    send_lights((pos == 1) & (rel == 2), (1, 3), 2)
+    send_lights(pos == 3, (3,), 2)
     relay((2, 2))
     relay((2, 3), (3, 0))
-    relay((3, 1))
-    arrived(1)
-    arrived(2)
-    for copy in news:
-        copy.wait_recv()
-    passed = [fresh_copy(4 + i, b + c, sib) for i, b in enumerate((dn - c, xn - c, yn - c))]
-    for copy in passed:
-        copy.start()
     for copy in sums:
         copy.wait()
     for k in range(1, tps):
         head = head + rs_recv[k - 1].astype(f32)
     attn_out[...] = head.astype(bf16)
-    summed = act_all[me_t].astype(f32) + head
+    summed = features(me_t) + head
     along = jnp.sum(summed * twist[...], -1, keepdims=True)
     energy = jnp.sum(summed * summed, -1, keepdims=True)
     lane = lax.broadcasted_iota(jnp.int32, (rows, HD), 1)
@@ -937,8 +959,7 @@
     scores = [
         tp_push(2 * (tps - 1), k, sc_all.at[me_t], sc_all.at[me_t]) for k in range(1, tps)
     ]
-    relay((3, 2))
-    arrived(3)
+    relay((3, 1))
     for copy in scores:
         copy.wait()
     both = sc_all[0]
@@ -976,6 +997,15 @@
         copy.start()
         lws.append(copy)
 
+    arrived(2)
+    arrived(1)
+    relay((3, 2))
+    for copy in news:
+        copy.wait_recv()
+    passed = [fresh_copy(4 + i, block, sib) for i, block in enumerate((dn, xn, yn))]
+    for copy in passed:
+        copy.start()
+    arrived(3)
     relay((3, 3))
     for copy in passed:
         copy.wait()
@@ -1063,20 +1093,24 @@
     hbm = pl.BlockSpec(memory_space=pl.ANY)
     dma = pltpu.SemaphoreType.DMA
     both = jax.ShapeDtypeStruct((2 * parts, span, kvw), bf16)
-    tab, chip_k, chip_v = pl.pallas_call(
-        functools.partial(plan_kernel, parts, doms, cap, HOT_CAP, steps, rows),
-        out_shape=(jax.ShapeDtypeStruct((8, HD), jnp.int32), both, both),
-        in_specs=[vmem, hbm, hbm],
-        out_specs=(vmem,) * 3,
+    tab, chip_k, chip_v, act_part = pl.pallas_call(
+        functools.partial(plan_kernel, parts, doms, tps, cap, HOT_CAP, steps, rows),
+        out_shape=(
+            jax.ShapeDtypeStruct((8, HD), jnp.int32), both, both,
+            jax.ShapeDtypeStruct((tps, EARLY * parts, width), bf16),
+        ),
+        in_specs=[vmem, hbm, hbm, hbm],
+        out_specs=(vmem,) * 4,
         scratch_shapes=[
             pltpu.VMEM((doms, 8, HD), f32),
-            dma((doms - 1,)), dma((doms - 1,)), dma((2,)), dma((2,)), dma((2,)),
+            dma((doms - 1,)), dma((doms - 1,)), dma((3,)), dma((2,)), dma((2,)),
+            dma((tps - 1,)), dma((tps - 1,)),
         ],
         compiler_params=pltpu.CompilerParams(
             collective_id=5, has_side_effects=True, vmem_limit_bytes=16 << 20
         ),
         name="plan",
-    )(copy_counts.reshape(1, parts), cache_keys, cache_values)
+    )(copy_counts.reshape(1, parts), activations.reshape(rows, width), cache_keys, cache_values)
 
     def hot_branch(hot):
         result = jax.ShapeDtypeStruct((parts, span + steps, kvw), bf16)
@@ -1086,10 +1120,10 @@
                 jax.ShapeDtypeStruct((rows, width), bf16), result, result,
                 jax.ShapeDtypeStruct((parts, HD), f32),
             ),
-            in_specs=[hbm, vmem] + [hbm] * 4 + [vmem] * 8 + [smem, vmem],
+            in_specs=[hbm, vmem, vmem] + [hbm] * 4 + [vmem] * 8 + [smem, vmem],
             out_specs=(vmem,) * 4,
             scratch_shapes=[
-                pltpu.VMEM((tps, rows, width), bf16),
+                pltpu.VMEM((tps, rows - EARLY * parts, width), bf16),
                 pltpu.VMEM(w_query.shape, bf16),
                 pltpu.VMEM(w_key.shape, bf16),
                 pltpu.VMEM(value_weight.shape, bf16),
@@ -1121,19 +1155,19 @@
         )
 
         def run(
-            act, gain, wq, wk, wv, wo, chip_k, chip_v, twist, tokens, table, prev, cosine,
-            sine, tab, ck, cv, counts,
+            act, act_part, gain, wq, wk, wv, wo, chip_k, chip_v, twist, tokens, table, prev,
+            cosine, sine, tab, ck, cv, counts,
         ):
             return call(
-                act, gain, wq, wk, wv, wo, chip_k, chip_v, twist, tokens, table, prev,
-                cosine, sine, tab, tab,
+                act, act_part, gain, wq, wk, wv, wo, chip_k, chip_v, twist, tokens, table,
+                prev, cosine, sine, tab, tab,
             )
 
         return run
 
     def every(
-        act, gain, wq, wk, wv, wo, chip_k, chip_v, twist, tokens, table, prev, cosine,
-        sine, tab, ck, cv, counts,
+        act, act_part, gain, wq, wk, wv, wo, chip_k, chip_v, twist, tokens, table, prev,
+        cosine, sine, tab, ck, cv, counts,
     ):
         reward = jnp.sum(table.reshape(-1)[tokens].astype(f32), 0)
         aux = jnp.stack([prev[0] + reward, counts.astype(f32)], 1)
@@ -1144,7 +1178,7 @@
     attn, new_k, new_v, out_lw = lax.switch(
         tab[4, 0],
         [hot_branch(hot) for hot in range(4)] + [every],
-        activations.reshape(rows, width), norm_gain.reshape(1, -1), w_query, w_key,
+        activations.reshape(rows, width), act_part, norm_gain.reshape(1, -1), w_query, w_key,
         value_weight, w_output, chip_k, chip_v, twist_vec.reshape(1, -1), tokens,
         twisting_table.reshape(-1, HD), previous_log_weights.reshape(1, parts),
         jnp.asarray(cosine), jnp.asarray(sine), tab, cache_keys, cache_values, copy_counts,

time: 65.1 us -> 57.8 us (0.89)
  Pallas kernels: 58.5 us -> 51 us
    pallas_call x2, Pallas kernels: 58.5 us -> 51 us  [the longest x1 39.8 us: run(): call(act, act_part, gain, wq, wk, wv, wo, chip_k, chip_v, twist, tokens,...]
    unnamed x13 -> x15, local copies, waits for them, and re-layouts: 3.06 us -> 3.06 us
where the time goes in v3:
time: 57.8 us; the launch traced here: 57.2 us
  Pallas kernels  51 us (88%)
  local copies, waits for them, and re-layouts  4.2 us (7%)
  between operations  1.4 us (2%)
    pallas_call x1, Pallas kernels, run(): call(act, act_part, gain, wq, wk, wv, wo, chip_k, chip_v, twist, tokens,...  39.8 us
    pallas_call x1, Pallas kernels, adaptive(): pl.pallas_call(functools.partial(plan_kernel, parts, doms, tps, cap, HOT_...  11.2 us
    unnamed x15, local copies, waits for them, and re-layouts  3.06 us

profile of v3, /device:TPU:0, one launch (start us, length us, event | category | flops | bytes accessed | tf_op | source)
XLA Modules:
  0.0 57.2 jit_solution(7589732145500299670)
XLA Ops:
  0.6 0.0 copy-start.2
  0.6 0.0 copy-start.3
  0.7 0.0 copy-start.7
  0.7 0.0 copy-start.8
  0.7 0.0 copy-start.9
  0.7 0.0 copy-start.11
  0.7 11.2 %plan.1 = (s32[8,128]{1,0:T(8,128)S(1)}, bf16[32,128,256]{2,1,0:T(8,128)(2,1)S(1)}, bf16[32,128,256]{2,1,0:T(8,128)(2,1)S(1)}, bf16[4,16,1024]{2,1,0:T(8,128)(2,1)S(1)}) custom-call(s32[1,16]{1,0:T(1,128)} %bitcast.43, bf16[64,1024]{1,0:T(8,128)(2,1)} %bitcast.22, bf16[16,128,256]{2,1,0:T(8,128)(2,1)} %ck.1, bf16[16,128,256]{2,1,0:T(8,128)(2,1)} %cv.1), custom_call_target="tpu_custom_call" | custom-call | tf_op jit(solution)/shard_map/plan/pallas_call | solution.py:1096
  11.9 0.5 slice.12
  13.1 0.0 copy-done.2
  13.1 0.0 copy-done.3
  13.1 0.0 copy-done.7
  13.1 0.0 copy-done.8
  13.2 0.0 copy-done.9
  13.2 0.0 copy-done.11
  13.2 40.3 %conditional.1 = (bf16[16,132,256]{2,1,0:T(8,128)(2,1)S(1)}, bf16[16,132,256]{2,1,0:T(8,128)(2,1)S(1)}, bf16[64,1024]{1,0:T(8,128)(2,1)S(1)}, f32[16,128]{1,0:T(8,128)S(1)}) conditional(s32[]{:T(128)} %bitcast.12, (bf16[128256]{0:T(1024)(128)(2,1)}, f32[16]{0:T(128)S(1)}, bf16[64,1024]{1,0:T(8,128)(2,1)S(1)}, ...), branch_computations={%region_0.0_spmd, %region_1.0_spmd, %region_2.0_spmd, %region_3.0_... | conditional | flops 1328 | bytes 71540168 | solution.py:1178
  13.2 39.8 %main0.1 = (bf16[64,1024]{1,0:T(8,128)(2,1)S(1)}, bf16[16,132,256]{2,1,0:T(8,128)(2,1)S(1)}, bf16[16,132,256]{2,1,0:T(8,128)(2,1)S(1)}, f32[16,128]{1,0:T(8,128)S(1)}) custom-call(bf16[64,1024]{1,0:T(8,128)(2,1)S(1)} %get-tuple-element.188.act, bf16[4,16,1024]{2,1,0:T(8,128)(2,1)S(1)} %get-tuple-element.189.act_part, f32[1,4096]{1,0:T(1,128)} %get-tuple-element.190.gain, ...), custom_call_target="tpu_custom_call" | custom-call | tf_op jit(solution)/shard_map/cond/branch_0_fun/main0/pallas_call | solution.py:1161
  53.5 0.6 %slice_reduce_fusion = f32[16]{0:T(128)} fusion(f32[16,128]{1,0:T(8,128)S(1)} %get-tuple-element.310), kind=kLoop, calls=%fused_computation.6 | loop fusion | bytes 128 | tf_op jit(solution)/shard_map/slice | solution.py:1186
  54.1 1.2 %copy.28 = bf16[16,132,256]{2,0,1:T(8,128)(2,1)} copy(bf16[16,132,256]{2,1,0:T(8,128)(2,1)S(1)} %get-tuple-element.320) | data formatting | bytes 2162688
  55.3 1.2 %copy.29 = bf16[16,132,256]{2,0,1:T(8,128)(2,1)} copy(bf16[16,132,256]{2,1,0:T(8,128)(2,1)S(1)} %get-tuple-element.321) | data formatting | bytes 2162688
  56.5 0.7 %copy.51 = bf16[4,16,1024]{2,1,0:T(8,128)(2,1)} copy(bf16[4,16,1024]{2,1,0:T(8,128)(2,1)S(1)} %bitcast.33) | data formatting | bytes 262144
Async XLA Ops:
  0.6 12.5 %copy-start.2 = (bf16[4096,256]{1,0:T(8,128)(2,1)S(1)}, bf16[4096,256]{1,0:T(8,128)(2,1)}, u32[]{:S(2)}) copy-start(bf16[4096,256]{1,0:T(8,128)(2,1)} %param.23) | copy-start | bytes 6291460
  0.6 12.5 %copy-start.3 = (bf16[4,16,1024]{2,1,0:T(8,128)(2,1)S(1)}, bf16[4,16,1024]{2,1,0:T(8,128)(2,1)}, u32[]{:S(2)}) copy-start(bf16[4,16,1024]{2,1,0:T(8,128)(2,1)} %param.20) | copy-start | bytes 393220
  0.7 12.5 %copy-start.7 = (f32[1024]{0:T(1024)S(1)}, f32[1024]{0:T(1024)}, u32[]{:S(2)}) copy-start(f32[1024]{0:T(1024)} %param.30) | copy-start | bytes 12292
  0.7 12.5 %copy-start.8 = (s32[4,16]{1,0:T(4,128)S(1)}, s32[4,16]{1,0:T(4,128)}, u32[]{:S(2)}) copy-start(s32[4,16]{1,0:T(4,128)} %param.28) | copy-start | bytes 772
  0.7 12.5 %copy-start.9 = (f32[16]{0:T(128)S(1)}, f32[16]{0:T(128)}, u32[]{:S(2)}) copy-start(f32[16]{0:T(128)} %param.31) | copy-start | bytes 196
  0.7 12.5 %copy-start.11 = (s32[16]{0:T(128)S(1)}, s32[16]{0:T(128)}, u32[]{:S(2)}) copy-start(s32[16]{0:T(128)} %param.32) | copy-start | bytes 196

commit v4 on v3

--- a/solution.py
+++ b/solution.py
@@ -612,16 +612,21 @@
     there_x = x + kind % 2 - 2 * x * (kind % 2)
     there_y = y + kind // 2 - 2 * y * (kind // 2)
     need_send = needs(2 * there_y + there_x)
+    kind = jnp.minimum(lane // 16, 2) + 1
+    there_x = x + kind % 2 - 2 * x * (kind % 2)
+    there_y = y + kind // 2 - 2 * y * (kind // 2)
+    need_fresh = needs(2 * there_y + there_x)
     need_here = needs(jnp.broadcast_to(chip, (whole, HD)))
     need_any = needs(lane % 4)
     before = (second < first) & (second // (2 * parts) == first // (2 * parts))
     places = total(
         before,
-        jnp.concatenate([u.astype(f32) for u in (need_send, need_here, need_any)], 1),
+        jnp.concatenate([u.astype(f32) for u in (need_send, need_here, need_any, need_fresh)], 1),
     ).astype(i32)
     place_send = places[:, :HD]
     place_here = places[:, HD : 2 * HD]
-    place_any = places[:, 2 * HD :]
+    place_any = places[:, 2 * HD : 3 * HD]
+    place_fresh = places[:, 3 * HD :]
     local_row = j % parts + parts * (owner % 2 + core - 2 * core * (owner % 2))
     half = cap // 2
     entry = lane % cap
@@ -641,11 +646,29 @@
     rank = lane * doms + me_d
     mine = (starts <= rank) & (rank < ends)
     index = jnp.sum(jnp.where(mine, value, 0).astype(f32), 0, keepdims=True)
+    deep = lane % 16 // steps
+    hit = need_fresh & (place_fresh == 2 * deep + core) & (lane < 48) & (deep < half)
+    hot = (owner == heavy) & (lane >= 64)
+    hot = hot & (j % parts == parts // 2 * core + (lane - 64) // steps)
+    hot = hot & (lane < 64 + parts // 2 * steps)
+    spot = local_row // parts * rows + j % parts
+    hit = (hit | hot) & (home == chip)
+    picks = jnp.where(hit, spot + lane % steps * parts + 1, 0).astype(f32)
+    picks = jnp.sum(picks, 0, keepdims=True).astype(i32) - 1
     wide = (lane // 8) * doms + me_d
-    old = jnp.sum((ends <= wide).astype(f32), 0, keepdims=True).astype(i32)
-    row = lax.broadcasted_iota(i32, (1, HD), 1)
-    target = (old // parts) * rows + (row % 8) * parts + old % parts
-    target = jnp.where(row % 8 < steps, target, -1)
+    step = lane % 8
+    spot = jnp.where(
+        away == 0,
+        spot + step * parts,
+        jnp.where(
+            light,
+            3 * rows + (away - 1) * 32 + place_here % 2 * 16 + place_here // 2 * steps + step,
+            2 * rows + j % parts * steps + step,
+        ),
+    )
+    chosen = (starts <= wide) & (wide < ends) & (step < steps)
+    target = jnp.where(chosen, spot + 1, 0).astype(f32)
+    target = jnp.sum(target, 0, keepdims=True).astype(i32) - 1
     room = jnp.where(home == heavy // 2, hot_cap, cap)
     over = jnp.max(
         (need_any & (place_any >= room)).astype(f32), (0, 1), keepdims=True
@@ -657,7 +680,8 @@
     tab[2:3, :] = jnp.broadcast_to(base, (1, HD))
     tab[3:4, :] = target
     tab[4:5, :] = jnp.broadcast_to(branch, (1, HD))
-    tab[5:8, :] = jnp.zeros((3, HD), i32)
+    tab[5:6, :] = picks
+    tab[6:8, :] = jnp.zeros((2, HD), i32)
     for copy in owns + swaps:
         copy.wait()
 
@@ -668,7 +692,7 @@
     cosine, sine, tab, tabv,
     attn_out, new_k, new_v, out_lw,
     act_all, wq_v, wk_v, wv_v, wo_v, all_k, all_v, send_k, send_v,
-    qs, cx, sc1, ctx_b, fresh_all, rs_send, rs_recv, sc_all, lw_all,
+    qs, cx, sc1, ctx_b, pair_f, hot_f, light_f, send_f, rs_send, rs_recv, sc_all, lw_all,
     loc, tp_send, tp_recv, lw_send, lw_recv,
     hv_send, hv_recv, li_send, li_recv, fr_send, fr_recv,
 ):
@@ -802,11 +826,13 @@
                 for which in range(2):
                     forward(i // chunk, which).start()
 
-    for k in (2, 1, 3):
-        for t in range(lane_rows):
-            at = tab[0, k * cap + lane_rows * c + t]
-            send_k[k - 1, t] = chip_k[at]
-            send_v[k - 1, t] = chip_v[at]
+    def gather(i, carry):
+        at = tab[0, (i // lane_rows + 1) * cap + lane_rows * c + i % lane_rows]
+        send_k[i // lane_rows, i % lane_rows] = chip_k[at]
+        send_v[i // lane_rows, i % lane_rows] = chip_v[at]
+        return carry
+
+    lax.fori_loop(0, 3 * lane_rows, gather, 0)
     send_lights((pos == 1) & (rel == 1), (1,), 2)
     send_lights((pos == 1) & (rel == 2), (2,), 2)
     send_lights((pos == 3) & (rel == 1), (2, 1), 2)
@@ -864,18 +890,33 @@
     load_k.wait()
     load_v.wait()
     keys = project(wk_v)
-    fresh = fresh_all.at[me_d]
+    fresh = pair_f.at[0]
     for g in range(groups):
         fresh[:, g * HD : (g + 1) * HD] = turn(keys[:, g * HD : (g + 1) * HD]).astype(bf16)
     fresh[:, kvw:] = project(wv_v).astype(bf16)
 
-    def fresh_copy(i, block, to):
-        area = fresh_all.at[block]
-        return push(area, area, fr_send.at[i], fr_recv.at[i], to, me_t)
-
-    news = [fresh_copy(i, me_d, to) for i, to in enumerate((dn, xn, yn, sib))]
-    for copy in news:
-        copy.start()
+    swap_f = push(fresh, pair_f.at[1], fr_send.at[0], fr_recv.at[0], sib, me_t)
+    swap_f.start()
+
+    def light_fresh(k):
+        return push(
+            send_f.at[k - 1], light_f.at[k - 1, c], fr_send.at[k], fr_recv.at[k],
+            (xn, yn, dn)[k - 1], me_t,
+        )
+
+    def hot_fresh(k):
+        return push(
+            send_f.at[pl.ds(4, 2)], hot_f.at[c], fr_send.at[3 + k], fr_recv.at[3 + k],
+            (xn, yn, dn)[k - 1], me_t,
+        )
+
+    def light_fresh_mirror(k):
+        area = light_f.at[k - 1, c]
+        return push(area, area, fr_send.at[6 + k], fr_recv.at[6 + k], sib, me_t)
+
+    def hot_fresh_mirror():
+        return push(hot_f.at[c], hot_f.at[c], fr_send.at[10], fr_recv.at[10], sib, me_t)
+
     load_q.wait()
     query = project(wq_v)
     for h in range(groups * per):
@@ -933,16 +974,53 @@
             preferred_element_type=f32,
         )
 
+    lane = lax.broadcasted_iota(jnp.int32, (rows, HD), 1)
+    line = lax.broadcasted_iota(jnp.int32, (rows, HD), 0)
+
+    def flat(column, start=0):
+        return jnp.sum(jnp.where(lane == line + start, column, 0.0), 0, keepdims=True)
+
+    count = table.shape[0]
+    deep = lax.broadcasted_iota(jnp.int32, (rows, parts), 0) % parts
+    broad = lax.broadcasted_iota(jnp.int32, (rows, parts), 1)
+    names = jnp.concatenate(
+        [jnp.broadcast_to(tokens[s : s + 1, :], (parts, parts)) for s in range(steps)], 0
+    )
+    name = jnp.sum(jnp.where(deep == broad, names, 0).astype(f32), -1, keepdims=True)
+    name = name.astype(jnp.int32)
+    entry = lax.broadcasted_iota(jnp.int32, (rows, count), 1)
+    found = jnp.dot(
+        (entry == name // HD).astype(f32).astype(bf16), table[...], preferred_element_type=f32
+    )
+    gift = flat(jnp.sum(jnp.where(lane == name % HD, found, 0.0), -1, keepdims=True))
+    lw_all[me_d] = jnp.full((8, HD), -jnp.inf, f32)
+
     sums = []
     for k in (2, 1, 3)[: tps - 1]:
         rs_send[k - 1] = mix((me_t + k) % tps).astype(bf16)
         sums.append(tp_push(tps - 1, k, rs_send.at[k - 1], rs_recv.at[k - 1]))
     head = mix(me_t)
+    swap_f.wait_recv()
+    pair = pair_f[...].reshape(2 * rows, 2 * kvw)
+    index = lax.broadcasted_iota(jnp.int32, (2 * rows, HD), 0)
+    pick = (index == tabv[5:6, :]).astype(f32).astype(bf16)
+    send_f[...] = lax.dot_general(
+        pick, pair, (((0,), (0,)), ((), ())), preferred_element_type=f32
+    ).astype(bf16).reshape(send_f.shape)
+    for k in (3, 1, 2):
+        light_fresh(k).start()
+
+    @pl.when(pos == 0)
+    def _():
+        hot_f[...] = jnp.zeros(hot_f.shape, bf16)
+        for k in (3, 1, 2):
+            hot_fresh(k).start()
+
     relay((1, 3), (2, 1))
     send_lights((pos == 0) & (c == 0), (2,), 1)
     send_lights((pos == 0) & (c == 1), (3, 1), 1)
-    send_lights((pos == 1) & (rel == 1), (2, 3), 2)
-    send_lights((pos == 1) & (rel == 2), (1, 3), 2)
+    send_lights((pos == 1) & (rel == 1), (3, 2), 2)
+    send_lights((pos == 1) & (rel == 2), (3, 1), 2)
     send_lights(pos == 3, (3,), 2)
     relay((2, 2))
     relay((2, 3), (3, 0))
@@ -954,8 +1032,7 @@
     summed = features(me_t) + head
     along = jnp.sum(summed * twist[...], -1, keepdims=True)
     energy = jnp.sum(summed * summed, -1, keepdims=True)
-    lane = lax.broadcasted_iota(jnp.int32, (rows, HD), 1)
-    sc_all[me_t] = jnp.where(lane < HD // 2, along, energy)
+    sc_all[me_t] = jnp.broadcast_to(flat(along) + flat(energy, HD // 2), (8, HD))
     scores = [
         tp_push(2 * (tps - 1), k, sc_all.at[me_t], sc_all.at[me_t]) for k in range(1, tps)
     ]
@@ -965,29 +1042,14 @@
     both = sc_all[0]
     for t in range(1, tps):
         both = both + sc_all[t]
-    score = both[:, :1] / jnp.sqrt(both[:, HD - 1 :] / (width * tps) + 1e-06)
-    total = score[:parts]
+    power = pltpu.roll(both, HD // 2, 1)
+    score = both / jnp.sqrt(power / (width * tps) + 1e-06)
+    score = jnp.where(lane[:8] < rows, score + gift, 0.0)
+    total = score
     for s in range(1, steps):
-        total = total + score[s * parts : (s + 1) * parts]
-    count = table.shape[0]
-    deep = lax.broadcasted_iota(jnp.int32, (rows, parts), 0) % parts
-    broad = lax.broadcasted_iota(jnp.int32, (rows, parts), 1)
-    names = jnp.concatenate(
-        [jnp.broadcast_to(tokens[s : s + 1, :], (parts, parts)) for s in range(steps)], 0
-    )
-    name = jnp.sum(jnp.where(deep == broad, names, 0).astype(f32), -1, keepdims=True)
-    name = name.astype(jnp.int32)
-    line = lax.broadcasted_iota(jnp.int32, (rows, count), 1)
-    found = jnp.dot(
-        (line == name // HD).astype(f32).astype(bf16), table[...], preferred_element_type=f32
-    )
-    gift = jnp.sum(jnp.where(lane == name % HD, found, 0.0), -1, keepdims=True)
-    for s in range(steps):
-        total = total + gift[s * parts : (s + 1) * parts]
-    past = jnp.where(deep[:parts] == broad[:parts], prev[...], 0.0)
-    total = total + jnp.sum(past, -1, keepdims=True)
-    mine = jnp.broadcast_to(total, (parts, HD))
-    lw_all[me_d] = mine
+        total = total + pltpu.roll(score, HD - s * parts, 1)
+    mine = total[:, :parts] + jnp.broadcast_to(prev[...], (8, parts))
+    lw_all[me_d, :, :parts] = mine
     lws = []
     for k in range(1, doms):
         copy = push(
@@ -1000,30 +1062,40 @@
     arrived(2)
     arrived(1)
     relay((3, 2))
-    for copy in news:
-        copy.wait_recv()
-    passed = [fresh_copy(4 + i, block, sib) for i, block in enumerate((dn, xn, yn))]
-    for copy in passed:
-        copy.start()
+    for k in (1, 2, 3):
+        light_fresh(k).wait_recv()
+        light_fresh_mirror(k).start()
+
+        @pl.when(rel == k)
+        def _():
+            hot_fresh(k).wait_recv()
+            hot_fresh_mirror().start()
+
     arrived(3)
     relay((3, 3))
-    for copy in passed:
-        copy.wait()
-    index = lax.broadcasted_iota(jnp.int32, (doms * rows, HD), 0)
+    for k in (1, 2, 3):
+        light_fresh_mirror(k).wait()
+
+    @pl.when(pos > 0)
+    def _():
+        hot_fresh_mirror().wait()
+
+    pool = jnp.concatenate(
+        [
+            pair_f[...].reshape(2 * rows, 2 * kvw),
+            hot_f[...].reshape(rows, 2 * kvw),
+            light_f[...].reshape(96, 2 * kvw),
+        ],
+        0,
+    )
+    index = lax.broadcasted_iota(jnp.int32, (3 * rows + 96, HD), 0)
     pick = (index == tabv[3:4, :]).astype(f32).astype(bf16)
     chosen = lax.dot_general(
-        pick, fresh_all[...].reshape(doms * rows, 2 * kvw),
-        (((0,), (0,)), ((), ())), preferred_element_type=f32,
+        pick, pool, (((0,), (0,)), ((), ())), preferred_element_type=f32
     ).astype(bf16)
     for i in range(parts):
         new_k[i, span:, :] = chosen[i * 8 : i * 8 + steps, :kvw]
         new_v[i, span:, :] = chosen[i * 8 : i * 8 + steps, kvw:]
-
-    for copy in lws:
-        copy.wait()
-    largest = jnp.max(lw_all[...], (0, 1), keepdims=True)[0]
-    mass = jnp.sum(jnp.exp(lw_all[...] - largest[None]), (0, 1), keepdims=True)[0]
-    out_lw[...] = mine - (largest + jnp.log(mass))
 
     both_k.wait()
     both_v.wait()
@@ -1042,10 +1114,20 @@
             for which in range(2):
                 mirror(q, which).wait()
 
-    for i in range(parts):
+    def place(i, carry):
         at = tab[1, i]
         new_k[i, :span, :] = all_k[at]
         new_v[i, :span, :] = all_v[at]
+        return carry
+
+    lax.fori_loop(0, parts, place, 0)
+
+    for copy in lws:
+        copy.wait()
+    every_lw = lw_all[:, 0, :]
+    largest = jnp.max(every_lw, (0, 1), keepdims=True)
+    mass = jnp.sum(jnp.exp(every_lw - largest), (0, 1), keepdims=True)
+    out_lw[...] = mine[:1] - (largest + jnp.log(mass))
 
     @pl.when(pos < 3)
     def _():
@@ -1063,8 +1145,14 @@
             for which in range(2):
                 light(k, which, 1).wait_send()
 
-    for copy in news:
-        copy.wait_send()
+    for k in (1, 2, 3):
+        light_fresh(k).wait_send()
+    swap_f.wait_send()
+
+    @pl.when(pos == 0)
+    def _():
+        for k in (1, 2, 3):
+            hot_fresh(k).wait_send()
 
 
 def adaptive(
@@ -1118,7 +1206,7 @@
             functools.partial(main_kernel, steps, parts, doms, tps, cap, HOT_CAP, hot),
             out_shape=(
                 jax.ShapeDtypeStruct((rows, width), bf16), result, result,
-                jax.ShapeDtypeStruct((parts, HD), f32),
+                jax.ShapeDtypeStruct((1, parts), f32),
             ),
             in_specs=[hbm, vmem, vmem] + [hbm] * 4 + [vmem] * 8 + [smem, vmem],
             out_specs=(vmem,) * 4,
@@ -1136,17 +1224,20 @@
                 pltpu.VMEM((groups, parts, pack, HD), f32),
                 pltpu.VMEM((groups, parts * pack, span), f32),
                 pltpu.VMEM((rows, qw), bf16),
-                pltpu.VMEM((doms, rows, 2 * kvw), bf16),
+                pltpu.VMEM((2, rows, 2 * kvw), bf16),
+                pltpu.VMEM((2, 2, 16, 2 * kvw), bf16),
+                pltpu.VMEM((3, 2, 16, 2 * kvw), bf16),
+                pltpu.VMEM((8, 16, 2 * kvw), bf16),
                 pltpu.VMEM((tps - 1, rows, width), bf16),
                 pltpu.VMEM((tps - 1, rows, width), bf16),
-                pltpu.VMEM((tps, rows, HD), f32),
-                pltpu.VMEM((doms, parts, HD), f32),
+                pltpu.VMEM((tps, 8, HD), f32),
+                pltpu.VMEM((doms, 8, HD), f32),
                 dma((9,)),
                 dma((3 * (tps - 1),)), dma((3 * (tps - 1),)),
                 dma((doms - 1,)), dma((doms - 1,)),
                 dma((16,)), dma((16,)),
                 dma((24,)), dma((24,)),
-                dma((7,)), dma((7,)),
+                dma((11,)), dma((11,)),
             ],
             compiler_params=pltpu.CompilerParams(
                 collective_id=hot, has_side_effects=True, vmem_limit_bytes=42 << 20
@@ -1171,9 +1262,10 @@
     ):
         reward = jnp.sum(table.reshape(-1)[tokens].astype(f32), 0)
         aux = jnp.stack([prev[0] + reward, counts.astype(f32)], 1)
-        return all_rows(
+        attn, new_k, new_v, out_lw = all_rows(
             steps, parts, act, gain, wq, wk, wv, wo, ck, cv, twist, aux, cosine, sine
         )
+        return attn, new_k, new_v, out_lw[:, 0].reshape(1, parts)
 
     attn, new_k, new_v, out_lw = lax.switch(
         tab[4, 0],
@@ -1183,11 +1275,11 @@
         twisting_table.reshape(-1, HD), previous_log_weights.reshape(1, parts),
         jnp.asarray(cosine), jnp.asarray(sine), tab, cache_keys, cache_values, copy_counts,
     )
-    return attn.reshape(steps, parts, width), new_k, new_v, out_lw[:, 0]
+    return attn.reshape(steps, parts, width), new_k, new_v, out_lw.reshape(parts)
 
 
 def solution(mesh):
-    body = adaptive if mesh.shape["dom"] == 8 else local
+    body = adaptive if (mesh.shape["dom"], mesh.shape["tp"]) == (8, 4) else local
     return jax.shard_map(
         body,
         mesh=mesh,

time: 57.8 us -> 56.3 us (0.974)
  Pallas kernels: 51 us -> 49.6 us
    pallas_call x1, Pallas kernels: 39.8 us -> 38.1 us  [run(): call(act, act_part, gain, wq, wk, wv, wo, chip_k, chip_v, twist, tokens,...]
    slice x1 -> x0, local copies, waits for them, and re-layouts: 0.63 us -> none  [adaptive(): return (attn.reshape(steps, parts, width), new_k, new_v, out_lw[:, 0])]
    unnamed x15 -> x16, local copies, waits for them, and re-layouts: 3.06 us -> 3.57 us
where the time goes in v4:
time: 56.3 us; the launch traced here: 55.6 us
  Pallas kernels  49.6 us (88%)
  local copies, waits for them, and re-layouts  4.09 us (7%)
  between operations  1.4 us (2%)
    pallas_call x1, Pallas kernels, run(): call(act, act_part, gain, wq, wk, wv, wo, chip_k, chip_v, twist, tokens,...  38.1 us
    pallas_call x1, Pallas kernels, adaptive(): pl.pallas_call(functools.partial(plan_kernel, parts, doms, tps, cap, HOT_...  11.5 us
    unnamed x16, local copies, waits for them, and re-layouts  3.57 us

profile of v4, /device:TPU:0, one launch (start us, length us, event | category | flops | bytes accessed | tf_op | source)
XLA Modules:
  0.0 55.6 jit_solution(15340613743909275494)
XLA Ops:
  0.6 0.0 copy-start.2
  0.6 0.0 copy-start.3
  0.7 0.0 copy-start.7
  0.7 0.0 copy-start.8
  0.7 0.0 copy-start.9
  0.7 0.0 copy-start.10
  0.7 11.5 %plan.1 = (s32[8,128]{1,0:T(8,128)S(1)}, bf16[32,128,256]{2,1,0:T(8,128)(2,1)S(1)}, bf16[32,128,256]{2,1,0:T(8,128)(2,1)S(1)}, bf16[4,16,1024]{2,1,0:T(8,128)(2,1)S(1)}) custom-call(s32[1,16]{1,0:T(1,128)} %bitcast.47, bf16[64,1024]{1,0:T(8,128)(2,1)} %bitcast.26, bf16[16,128,256]{2,1,0:T(8,128)(2,1)} %ck.1, bf16[16,128,256]{2,1,0:T(8,128)(2,1)} %cv.1), custom_call_target="tpu_custom_call" | custom-call | tf_op jit(solution)/shard_map/plan/pallas_call | solution.py:1184
  12.2 0.5 slice.6
  13.3 0.0 copy-done.2
  13.3 0.0 copy-done.3
  13.3 0.0 copy-done.7
  13.4 0.0 copy-done.8
  13.4 0.0 copy-done.9
  13.4 0.0 copy-done.10
  13.4 38.7 %conditional.1 = (bf16[16,132,256]{2,1,0:T(8,128)(2,1)S(1)}, bf16[16,132,256]{2,1,0:T(8,128)(2,1)S(1)}, f32[16]{0:T(128)S(1)}, bf16[64,1024]{1,0:T(8,128)(2,1)S(1)}) conditional(s32[]{:T(128)} %bitcast.16, (bf16[128256]{0:T(1024)(128)(2,1)}, f32[16]{0:T(128)S(1)}, bf16[64,1024]{1,0:T(8,128)(2,1)S(1)}, ...), branch_computations={%region_0.0_spmd, %region_1.0_spmd, %region_2.0_spmd, %region_3.0_... | conditional | flops 1328 | bytes 71507504 | solution.py:1270
  13.6 38.1 %main2.1 = (bf16[64,1024]{1,0:T(8,128)(2,1)S(1)}, bf16[16,132,256]{2,1,0:T(8,128)(2,1)S(1)}, bf16[16,132,256]{2,1,0:T(8,128)(2,1)S(1)}, f32[1,16]{1,0:T(1,128)S(1)}) custom-call(bf16[64,1024]{1,0:T(8,128)(2,1)S(1)} %get-tuple-element.228.act, bf16[4,16,1024]{2,1,0:T(8,128)(2,1)S(1)} %get-tuple-element.229.act_part, f32[1,4096]{1,0:T(1,128)} %get-tuple-element.230.gain, ...), custom_call_target="tpu_custom_call" | custom-call | tf_op jit(solution)/shard_map/cond/branch_2_fun/main2/pallas_call | solution.py:1252
  52.1 1.2 %copy.28 = bf16[16,132,256]{2,0,1:T(8,128)(2,1)} copy(bf16[16,132,256]{2,1,0:T(8,128)(2,1)S(1)} %get-tuple-element.320) | data formatting | bytes 2162688
  53.3 1.2 %copy.29 = bf16[16,132,256]{2,0,1:T(8,128)(2,1)} copy(bf16[16,132,256]{2,1,0:T(8,128)(2,1)S(1)} %get-tuple-element.321) | data formatting | bytes 2162688
  54.5 0.7 %copy.52 = bf16[4,16,1024]{2,1,0:T(8,128)(2,1)} copy(bf16[4,16,1024]{2,1,0:T(8,128)(2,1)S(1)} %bitcast.37) | data formatting | bytes 262144
  55.1 0.5 copy.53
Async XLA Ops:
  0.6 12.7 %copy-start.2 = (bf16[4096,256]{1,0:T(8,128)(2,1)S(1)}, bf16[4096,256]{1,0:T(8,128)(2,1)}, u32[]{:S(2)}) copy-start(bf16[4096,256]{1,0:T(8,128)(2,1)} %param.23) | copy-start | bytes 6291460
  0.6 12.7 %copy-start.3 = (bf16[4,16,1024]{2,1,0:T(8,128)(2,1)S(1)}, bf16[4,16,1024]{2,1,0:T(8,128)(2,1)}, u32[]{:S(2)}) copy-start(bf16[4,16,1024]{2,1,0:T(8,128)(2,1)} %param.20) | copy-start | bytes 393220
  0.7 12.7 %copy-start.7 = (f32[1024]{0:T(1024)S(1)}, f32[1024]{0:T(1024)}, u32[]{:S(2)}) copy-start(f32[1024]{0:T(1024)} %param.30) | copy-start | bytes 12292
  0.7 12.7 %copy-start.8 = (s32[4,16]{1,0:T(4,128)S(1)}, s32[4,16]{1,0:T(4,128)}, u32[]{:S(2)}) copy-start(s32[4,16]{1,0:T(4,128)} %param.28) | copy-start | bytes 772
  0.7 12.7 %copy-start.9 = (f32[16]{0:T(128)S(1)}, f32[16]{0:T(128)}, u32[]{:S(2)}) copy-start(f32[16]{0:T(128)} %param.31) | copy-start | bytes 196
  0.7 12.7 %copy-start.10 = (s32[16]{0:T(128)S(1)}, s32[16]{0:T(128)}, u32[]{:S(2)}) copy-start(s32[16]{0:T(128)} %param.32) | copy-start | bytes 196

commit v5 on v4

--- a/solution.py
+++ b/solution.py
@@ -424,22 +424,23 @@
     put_v.wait()
 
 
-def select_kernel(parts, steps, anc, fresh_sel, all_k, all_v, new_k, new_v, sem):
-    span = all_k.shape[2]
-    width = all_k.shape[3]
+def select_kernel(
+    parts, anc, fresh_sel, attn, lw, all_k, all_v,
+    out_attn, new_k, new_v, chosen, out_lw, sem,
+):
     copies = []
     for i in range(parts):
         a = anc[0, i]
         d, n = a // parts, a % parts
         for which, (src, dst) in enumerate(((all_k, new_k), (all_v, new_v))):
-            copy = pltpu.make_async_copy(
-                src.at[d, n], dst.at[i, pl.ds(0, span)], sem.at[2 * i + which]
-            )
+            copy = pltpu.make_async_copy(src.at[d, n], dst.at[i], sem.at[2 * i + which])
             copy.start()
             copies.append(copy)
-    for i in range(parts):
-        new_k[i, span:, :] = fresh_sel[i * 8 : i * 8 + steps, :width]
-        new_v[i, span:, :] = fresh_sel[i * 8 : i * 8 + steps, width:]
+    chosen[...] = fresh_sel[...]
+    out_attn[...] = attn[...]
+    row = lax.broadcasted_iota(jnp.int32, (parts, parts), 0)
+    col = lax.broadcasted_iota(jnp.int32, (parts, parts), 1)
+    out_lw[...] = jnp.sum(jnp.where(row == col, lw[:, :1], 0.0), 0, keepdims=True)
     for copy in copies:
         copy.wait()
 
@@ -501,17 +502,20 @@
         ),
         name="layer",
     )(act, gain, wq, wk, wv, wo, ck, cv, twist, aux, cosine, sine)
-    result = jax.ShapeDtypeStruct((parts, span + steps, kvw), bf16)
-    new_k, new_v = pl.pallas_call(
-        functools.partial(select_kernel, parts, steps),
-        out_shape=(result, result),
-        in_specs=[pl.BlockSpec(memory_space=pltpu.SMEM), vmem, hbm, hbm],
-        out_specs=(vmem, vmem),
+    result = jax.ShapeDtypeStruct((parts, span, kvw), bf16)
+    return pl.pallas_call(
+        functools.partial(select_kernel, parts),
+        out_shape=(
+            jax.ShapeDtypeStruct((rows, width), bf16), result, result,
+            jax.ShapeDtypeStruct((HD, 2 * kvw), bf16),
+            jax.ShapeDtypeStruct((1, parts), f32),
+        ),
+        in_specs=[pl.BlockSpec(memory_space=pltpu.SMEM), vmem, vmem, vmem, hbm, hbm],
+        out_specs=(vmem,) * 5,
         scratch_shapes=[pltpu.SemaphoreType.DMA((2 * parts,))],
         compiler_params=pltpu.CompilerParams(vmem_limit_bytes=8 << 20),
         name="select",
-    )(anc, fresh_sel, all_k, all_v)
-    return attn, new_k, new_v, out_lw
+    )(anc, fresh_sel, attn, out_lw, all_k, all_v)
 
 
 def plan_kernel(
@@ -690,7 +694,7 @@
     steps, parts, doms, tps, cap, hot_cap, hot,
     act, act_part, gain, wq, wk, wv, wo, chip_k, chip_v, twist, tokens, table, prev,
     cosine, sine, tab, tabv,
-    attn_out, new_k, new_v, out_lw,
+    attn_out, new_k, new_v, chosen, out_lw,
     act_all, wq_v, wk_v, wv_v, wo_v, all_k, all_v, send_k, send_v,
     qs, cx, sc1, ctx_b, pair_f, hot_f, light_f, send_f, rs_send, rs_recv, sc_all, lw_all,
     loc, tp_send, tp_recv, lw_send, lw_recv,
@@ -1090,12 +1094,9 @@
     )
     index = lax.broadcasted_iota(jnp.int32, (3 * rows + 96, HD), 0)
     pick = (index == tabv[3:4, :]).astype(f32).astype(bf16)
-    chosen = lax.dot_general(
+    chosen[...] = lax.dot_general(
         pick, pool, (((0,), (0,)), ((), ())), preferred_element_type=f32
     ).astype(bf16)
-    for i in range(parts):
-        new_k[i, span:, :] = chosen[i * 8 : i * 8 + steps, :kvw]
-        new_v[i, span:, :] = chosen[i * 8 : i * 8 + steps, kvw:]
 
     both_k.wait()
     both_v.wait()
@@ -1116,8 +1117,8 @@
 
     def place(i, carry):
         at = tab[1, i]
-        new_k[i, :span, :] = all_k[at]
-        new_v[i, :span, :] = all_v[at]
+        new_k[i] = all_k[at]
+        new_v[i] = all_v[at]
         return carry
 
     lax.fori_loop(0, parts, place, 0)
@@ -1153,6 +1154,34 @@
     def _():
         for k in (1, 2, 3):
             hot_fresh(k).wait_send()
+
+
+def finish_kernel(
+    parts, steps, rows_k, rows_v, chosen, attn, lw,
+    out_k, out_v, out_attn, out_lw, buf_k, buf_v, sem,
+):
+    span, width = rows_k.shape[1:]
+    group = 32
+    copies = [pltpu.make_async_copy(attn, out_attn, sem.at[0])]
+    copies[0].start()
+
+    def send(buf, out, start, size):
+        copy = pltpu.make_async_copy(
+            buf.at[pl.ds(start, size)], out.at[pl.ds(start, size)], sem.at[len(copies)]
+        )
+        copy.start()
+        copies.append(copy)
+
+    for which, (src, buf, out) in enumerate(((rows_k, buf_k, out_k), (rows_v, buf_v, out_v))):
+        for g in range(0, span, group):
+            buf[g : g + group] = jnp.transpose(src[:, g : g + group, :], (1, 0, 2))
+            send(buf, out, g, group)
+        tail = chosen[:, which * width : (which + 1) * width].reshape(parts, 8, width)
+        buf[span:] = jnp.transpose(tail, (1, 0, 2))[:steps]
+        send(buf, out, span, steps)
+    out_lw[...] = lw[...]
+    for copy in copies:
+        copy.wait()
 
 
 def adaptive(
@@ -1201,15 +1230,16 @@
     )(copy_counts.reshape(1, parts), activations.reshape(rows, width), cache_keys, cache_values)
 
     def hot_branch(hot):
-        result = jax.ShapeDtypeStruct((parts, span + steps, kvw), bf16)
+        result = jax.ShapeDtypeStruct((parts, span, kvw), bf16)
         call = pl.pallas_call(
             functools.partial(main_kernel, steps, parts, doms, tps, cap, HOT_CAP, hot),
             out_shape=(
                 jax.ShapeDtypeStruct((rows, width), bf16), result, result,
+                jax.ShapeDtypeStruct((HD, 2 * kvw), bf16),
                 jax.ShapeDtypeStruct((1, parts), f32),
             ),
             in_specs=[hbm, vmem, vmem] + [hbm] * 4 + [vmem] * 8 + [smem, vmem],
-            out_specs=(vmem,) * 4,
+            out_specs=(vmem,) * 5,
             scratch_shapes=[
                 pltpu.VMEM((tps, rows - EARLY * parts, width), bf16),
                 pltpu.VMEM(w_query.shape, bf16),
@@ -1240,7 +1270,7 @@
                 dma((11,)), dma((11,)),
             ],
             compiler_params=pltpu.CompilerParams(
-                collective_id=hot, has_side_effects=True, vmem_limit_bytes=42 << 20
+                collective_id=hot, has_side_effects=True, vmem_limit_bytes=40 << 20
             ),
             name=f"main{hot}",
         )
@@ -1249,10 +1279,11 @@
             act, act_part, gain, wq, wk, wv, wo, chip_k, chip_v, twist, tokens, table, prev,
             cosine, sine, tab, ck, cv, counts,
         ):
-            return call(
+            attn, new_k, new_v, chosen, out_lw = call(
                 act, act_part, gain, wq, wk, wv, wo, chip_k, chip_v, twist, tokens, table,
                 prev, cosine, sine, tab, tab,
             )
+            return new_k, new_v, attn, chosen, out_lw
 
         return run
 
@@ -1262,12 +1293,12 @@
     ):
         reward = jnp.sum(table.reshape(-1)[tokens].astype(f32), 0)
         aux = jnp.stack([prev[0] + reward, counts.astype(f32)], 1)
-        attn, new_k, new_v, out_lw = all_rows(
+        attn, new_k, new_v, chosen, out_lw = all_rows(
             steps, parts, act, gain, wq, wk, wv, wo, ck, cv, twist, aux, cosine, sine
         )
-        return attn, new_k, new_v, out_lw[:, 0].reshape(1, parts)
-
-    attn, new_k, new_v, out_lw = lax.switch(
+        return new_k, new_v, attn, chosen, out_lw
+
+    rows_k, rows_v, attn, chosen, out_lw = lax.switch(
         tab[4, 0],
         [hot_branch(hot) for hot in range(4)] + [every],
         activations.reshape(rows, width), act_part, norm_gain.reshape(1, -1), w_query, w_key,
@@ -1275,7 +1306,25 @@
         twisting_table.reshape(-1, HD), previous_log_weights.reshape(1, parts),
         jnp.asarray(cosine), jnp.asarray(sine), tab, cache_keys, cache_values, copy_counts,
     )
-    return attn.reshape(steps, parts, width), new_k, new_v, out_lw.reshape(parts)
+    result = jax.ShapeDtypeStruct((span + steps, parts, kvw), bf16)
+    new_k, new_v, attn, out_lw = pl.pallas_call(
+        functools.partial(finish_kernel, parts, steps),
+        out_shape=(
+            result, result, jax.ShapeDtypeStruct((rows, width), bf16),
+            jax.ShapeDtypeStruct((1, parts), f32),
+        ),
+        in_specs=[vmem] * 5,
+        out_specs=(hbm, hbm, hbm, vmem),
+        scratch_shapes=[
+            pltpu.VMEM(result.shape, bf16), pltpu.VMEM(result.shape, bf16), dma((11,)),
+        ],
+        compiler_params=pltpu.CompilerParams(vmem_limit_bytes=8 << 20),
+        name="finish",
+    )(rows_k, rows_v, chosen, attn, out_lw)
+    return (
+        attn.reshape(steps, parts, width), jnp.transpose(new_k, (1, 0, 2)),
+        jnp.transpose(new_v, (1, 0, 2)), out_lw.reshape(parts),
+    )
 
 
 def solution(mesh):

time: 56.3 us -> 54.5 us (0.968)
  local copies, waits for them, and re-layouts: 4.09 us -> 0.54 us
  Pallas kernels: 49.6 us -> 51.6 us
    unnamed x16 -> x14, local copies, waits for them, and re-layouts: 3.57 us -> 0.03 us
    pallas_call x0 -> x1, Pallas kernels: none -> 1.99 us  [adaptive(): pl.pallas_call(functools.partial(finish_kernel, parts, steps), out_shape=...]
where the time goes in v5:
time: 54.5 us; the launch traced here: 54.3 us
  Pallas kernels  51.6 us (95%)
  between operations  1.63 us (3%)
  loops' own time  0.56 us (1%)
    pallas_call x1, Pallas kernels, run(): call(act, act_part, gain, wq, wk, wv, wo, chip_k, chip_v, twist, tokens,...  38.1 us
    pallas_call x1, Pallas kernels, adaptive(): pl.pallas_call(functools.partial(plan_kernel, parts, doms, tps, cap, HOT_...  11.5 us
    pallas_call x1, Pallas kernels, adaptive(): pl.pallas_call(functools.partial(finish_kernel, parts, steps), out_shape=...  1.99 us

profile of v5, /device:TPU:0, one launch (start us, length us, event | category | flops | bytes accessed | tf_op | source)
XLA Modules:
  0.0 54.3 jit_solution(14959930872030147970)
XLA Ops:
  0.6 0.0 copy-start.8
  0.6 0.0 copy-start.7
  0.7 0.0 copy-start.6
  0.7 0.0 copy-start.2
  0.7 0.0 copy-start.5
  0.7 0.0 copy-start.4
  0.7 0.0 copy-start.3
  0.7 11.5 %plan.1 = (s32[8,128]{1,0:T(8,128)S(1)}, bf16[32,128,256]{2,1,0:T(8,128)(2,1)S(1)}, bf16[32,128,256]{2,1,0:T(8,128)(2,1)S(1)}, bf16[4,16,1024]{2,1,0:T(8,128)(2,1)S(1)}) custom-call(s32[1,16]{1,0:T(1,128)} %bitcast.45, bf16[64,1024]{1,0:T(8,128)(2,1)} %bitcast.25, bf16[16,128,256]{2,1,0:T(8,128)(2,1)} %ck.1, bf16[16,128,256]{2,1,0:T(8,128)(2,1)} %cv.1), custom_call_target="tpu_custom_call" | custom-call | tf_op jit(solution)/shard_map/plan/pallas_call | solution.py:1213
  12.2 0.5 slice.3
  13.3 0.0 copy-done.8
  13.4 0.0 copy-done.7
  13.4 0.0 copy-done.6
  13.4 0.0 copy-done.2
  13.4 0.0 copy-done.5
  13.4 0.0 copy-done.4
  13.4 0.0 copy-done.3
  13.4 38.7 %conditional.1 = (bf16[16,128,256]{2,1,0:T(8,128)(2,1)S(1)}, bf16[16,128,256]{2,1,0:T(8,128)(2,1)S(1)}, bf16[64,1024]{1,0:T(8,128)(2,1)S(1)}, bf16[128,512]{1,0:T(8,128)(2,1)S(1)}, f32[1,16]{1,0:T(1,128)S(1)}) conditional(s32[]{:T(128)} %bitcast.12, (bf16[128256]{0:T(1024)(128)(2,1)}, f32[16]{0:T(128)S(1)}, ...), branch_computations={%region_0.0_spmd, %region_1.0_spmd, %region_2.0_spmd, %region_3.0_... | conditional | flops 1328 | bytes 67116392 | solution.py:1301
  13.7 38.1 %main2.1 = (bf16[64,1024]{1,0:T(8,128)(2,1)S(1)}, bf16[16,128,256]{2,1,0:T(8,128)(2,1)S(1)}, bf16[16,128,256]{2,1,0:T(8,128)(2,1)S(1)}, bf16[128,512]{1,0:T(8,128)(2,1)S(1)}, f32[1,16]{1,0:T(1,128)S(1)}) custom-call(bf16[64,1024]{1,0:T(8,128)(2,1)S(1)} %get-tuple-element.208.act, bf16[4,16,1024]{2,1,0:T(8,128)(2,1)S(1)} %get-tuple-element.209.act_part, ...), custom_call_target="tpu_custom_call" | custom-call | tf_op jit(solution)/shard_map/cond/branch_2_fun/main2/pallas_call | solution.py:1282
  52.1 2.0 %finish.1 = (bf16[132,16,256]{2,1,0:T(8,128)(2,1)}, bf16[132,16,256]{2,1,0:T(8,128)(2,1)}, bf16[64,1024]{1,0:T(8,128)(2,1)}, f32[1,16]{1,0:T(1,128)}) custom-call(bf16[16,128,256]{2,1,0:T(8,128)(2,1)S(1)} %get-tuple-element.297.rows_k, bf16[16,128,256]{2,1,0:T(8,128)(2,1)S(1)} %get-tuple-element.298.rows_v, bf16[128,512]{1,0:T(8,128)(2,1)S(1)} %get-tuple-element.299.chosen, ...), custom_call_target="tpu_custom_call" | custom-call | tf_op jit(solution)/shard_map/finish/pallas_call | solution.py:1310
Async XLA Ops:
  0.6 12.7 %copy-start.8 = (s32[16]{0:T(128)S(1)}, s32[16]{0:T(128)}, u32[]{:S(2)}) copy-start(s32[16]{0:T(128)} %param.32) | copy-start | bytes 196
  0.6 12.7 %copy-start.7 = (f32[16]{0:T(128)S(1)}, f32[16]{0:T(128)}, u32[]{:S(2)}) copy-start(f32[16]{0:T(128)} %param.31) | copy-start | bytes 196
  0.7 12.7 %copy-start.6 = (s32[4,16]{1,0:T(4,128)S(1)}, s32[4,16]{1,0:T(4,128)}, u32[]{:S(2)}) copy-start(s32[4,16]{1,0:T(4,128)} %param.28) | copy-start | bytes 772
  0.7 12.7 %copy-start.2 = (bf16[4096,256]{1,0:T(8,128)(2,1)S(1)}, bf16[4096,256]{1,0:T(8,128)(2,1)}, u32[]{:S(2)}) copy-start(bf16[4096,256]{1,0:T(8,128)(2,1)} %param.23) | copy-start | bytes 6291460
  0.7 12.7 %copy-start.5 = (f32[1024]{0:T(1024)S(1)}, f32[1024]{0:T(1024)}, u32[]{:S(2)}) copy-start(f32[1024]{0:T(1024)} %param.30) | copy-start | bytes 12292
  0.7 12.7 %copy-start.4 = (f32[4096]{0:T(1024)S(1)}, f32[4096]{0:T(1024)}, u32[]{:S(2)}) copy-start(f32[4096]{0:T(1024)} %param.21) | copy-start | bytes 49156
  0.7 12.7 %copy-start.3 = (bf16[4,16,1024]{2,1,0:T(8,128)(2,1)S(1)}, bf16[4,16,1024]{2,1,0:T(8,128)(2,1)}, u32[]{:S(2)}) copy-start(bf16[4,16,1024]{2,1,0:T(8,128)(2,1)} %param.20) | copy-start | bytes 393220

commit v6 on v5

--- a/solution.py
+++ b/solution.py
@@ -929,6 +929,9 @@
         for s in range(steps):
             qs[g, :, s * per + j, :] = turned[s * parts : (s + 1) * parts]
     relay((1, 2), (2, 0))
+    send_lights((pos == 0) & (c == 0), (2,), 1)
+    send_lights((pos == 0) & (c == 1), (3, 1), 1)
+    send_lights(pos == 3, (3,), 2)
 
     lines = parts * pack
     row = lax.broadcasted_iota(jnp.int32, (lines, rows), 0)
@@ -1021,11 +1024,8 @@
             hot_fresh(k).start()
 
     relay((1, 3), (2, 1))
-    send_lights((pos == 0) & (c == 0), (2,), 1)
-    send_lights((pos == 0) & (c == 1), (3, 1), 1)
     send_lights((pos == 1) & (rel == 1), (3, 2), 2)
     send_lights((pos == 1) & (rel == 2), (3, 1), 2)
-    send_lights(pos == 3, (3,), 2)
     relay((2, 2))
     relay((2, 3), (3, 0))
     for copy in sums:

time: 54.5 us -> 55.1 us (1.011)
  Pallas kernels: 51.6 us -> 52.2 us
    pallas_call x1, Pallas kernels: 38.1 us -> 38.7 us  [run(): call(act, act_part, gain, wq, wk, wv, wo, chip_k, chip_v, twist, tokens,...]
where the time goes in v6:
time: 55.1 us; the launch traced here: 54.9 us
  Pallas kernels  52.2 us (95%)
  between operations  1.63 us (3%)
    pallas_call x1, Pallas kernels, run(): call(act, act_part, gain, wq, wk, wv, wo, chip_k, chip_v, twist, tokens,...  38.7 us
    pallas_call x1, Pallas kernels, adaptive(): pl.pallas_call(functools.partial(plan_kernel, parts, doms, tps, cap, HOT_...  11.5 us
    pallas_call x1, Pallas kernels, adaptive(): pl.pallas_call(functools.partial(finish_kernel, parts, steps), out_shape=...  1.99 us

profile of v6, /device:TPU:0, one launch (start us, length us, event | category | flops | bytes accessed | tf_op | source)
XLA Modules:
  0.0 54.9 jit_solution(15015355403785414427)
XLA Ops:
  0.6 0.0 copy-start.8
  0.6 0.0 copy-start.7
  0.7 0.0 copy-start.6
  0.7 0.0 copy-start.2
  0.7 0.0 copy-start.5
  0.7 0.0 copy-start.4
  0.7 0.0 copy-start.3
  0.7 11.5 %plan.1 = (s32[8,128]{1,0:T(8,128)S(1)}, bf16[32,128,256]{2,1,0:T(8,128)(2,1)S(1)}, bf16[32,128,256]{2,1,0:T(8,128)(2,1)S(1)}, bf16[4,16,1024]{2,1,0:T(8,128)(2,1)S(1)}) custom-call(s32[1,16]{1,0:T(1,128)} %bitcast.45, bf16[64,1024]{1,0:T(8,128)(2,1)} %bitcast.25, bf16[16,128,256]{2,1,0:T(8,128)(2,1)} %ck.1, bf16[16,128,256]{2,1,0:T(8,128)(2,1)} %cv.1), custom_call_target="tpu_custom_call" | custom-call | tf_op jit(solution)/shard_map/plan/pallas_call | solution.py:1213
  12.2 0.5 slice.3
  13.3 0.0 copy-done.8
  13.4 0.0 copy-done.7
  13.4 0.0 copy-done.6
  13.4 0.0 copy-done.2
  13.4 0.0 copy-done.5
  13.4 0.0 copy-done.4
  13.4 0.0 copy-done.3
  13.4 39.3 %conditional.1 = (bf16[16,128,256]{2,1,0:T(8,128)(2,1)S(1)}, bf16[16,128,256]{2,1,0:T(8,128)(2,1)S(1)}, bf16[64,1024]{1,0:T(8,128)(2,1)S(1)}, bf16[128,512]{1,0:T(8,128)(2,1)S(1)}, f32[1,16]{1,0:T(1,128)S(1)}) conditional(s32[]{:T(128)} %bitcast.12, (bf16[128256]{0:T(1024)(128)(2,1)}, f32[16]{0:T(128)S(1)}, ...), branch_computations={%region_0.0_spmd, %region_1.0_spmd, %region_2.0_spmd, %region_3.0_... | conditional | flops 1328 | bytes 67116392 | solution.py:1301
  13.4 38.7 %main1.1 = (bf16[64,1024]{1,0:T(8,128)(2,1)S(1)}, bf16[16,128,256]{2,1,0:T(8,128)(2,1)S(1)}, bf16[16,128,256]{2,1,0:T(8,128)(2,1)S(1)}, bf16[128,512]{1,0:T(8,128)(2,1)S(1)}, f32[1,16]{1,0:T(1,128)S(1)}) custom-call(bf16[64,1024]{1,0:T(8,128)(2,1)S(1)} %get-tuple-element.187.act, bf16[4,16,1024]{2,1,0:T(8,128)(2,1)S(1)} %get-tuple-element.188.act_part, ...), custom_call_target="tpu_custom_call" | custom-call | tf_op jit(solution)/shard_map/cond/branch_1_fun/main1/pallas_call | solution.py:1282
  52.7 2.0 %finish.1 = (bf16[132,16,256]{2,1,0:T(8,128)(2,1)}, bf16[132,16,256]{2,1,0:T(8,128)(2,1)}, bf16[64,1024]{1,0:T(8,128)(2,1)}, f32[1,16]{1,0:T(1,128)}) custom-call(bf16[16,128,256]{2,1,0:T(8,128)(2,1)S(1)} %get-tuple-element.297.rows_k, bf16[16,128,256]{2,1,0:T(8,128)(2,1)S(1)} %get-tuple-element.298.rows_v, bf16[128,512]{1,0:T(8,128)(2,1)S(1)} %get-tuple-element.299.chosen, ...), custom_call_target="tpu_custom_call" | custom-call | tf_op jit(solution)/shard_map/finish/pallas_call | solution.py:1310
Async XLA Ops:
  0.6 12.7 %copy-start.8 = (s32[16]{0:T(128)S(1)}, s32[16]{0:T(128)}, u32[]{:S(2)}) copy-start(s32[16]{0:T(128)} %param.32) | copy-start | bytes 196
  0.6 12.7 %copy-start.7 = (f32[16]{0:T(128)S(1)}, f32[16]{0:T(128)}, u32[]{:S(2)}) copy-start(f32[16]{0:T(128)} %param.31) | copy-start | bytes 196
  0.7 12.7 %copy-start.6 = (s32[4,16]{1,0:T(4,128)S(1)}, s32[4,16]{1,0:T(4,128)}, u32[]{:S(2)}) copy-start(s32[4,16]{1,0:T(4,128)} %param.28) | copy-start | bytes 772
  0.7 12.7 %copy-start.2 = (bf16[4096,256]{1,0:T(8,128)(2,1)S(1)}, bf16[4096,256]{1,0:T(8,128)(2,1)}, u32[]{:S(2)}) copy-start(bf16[4096,256]{1,0:T(8,128)(2,1)} %param.23) | copy-start | bytes 6291460
  0.7 12.7 %copy-start.5 = (f32[1024]{0:T(1024)S(1)}, f32[1024]{0:T(1024)}, u32[]{:S(2)}) copy-start(f32[1024]{0:T(1024)} %param.30) | copy-start | bytes 12292
  0.7 12.7 %copy-start.4 = (f32[4096]{0:T(1024)S(1)}, f32[4096]{0:T(1024)}, u32[]{:S(2)}) copy-start(f32[4096]{0:T(1024)} %param.21) | copy-start | bytes 49156
  0.7 12.7 %copy-start.3 = (bf16[4,16,1024]{2,1,0:T(8,128)(2,1)S(1)}, bf16[4,16,1024]{2,1,0:T(8,128)(2,1)}, u32[]{:S(2)}) copy-start(bf16[4,16,1024]{2,1,0:T(8,128)(2,1)} %param.20) | copy-start | bytes 393220

commit v7 on v6

--- a/solution.py
+++ b/solution.py
@@ -929,6 +929,7 @@
         for s in range(steps):
             qs[g, :, s * per + j, :] = turned[s * parts : (s + 1) * parts]
     relay((1, 2), (2, 0))
+    send_lights((pos == 1) & (rel == 1), (3,), 2)
     send_lights((pos == 0) & (c == 0), (2,), 1)
     send_lights((pos == 0) & (c == 1), (3, 1), 1)
     send_lights(pos == 3, (3,), 2)
@@ -1024,7 +1025,7 @@
             hot_fresh(k).start()
 
     relay((1, 3), (2, 1))
-    send_lights((pos == 1) & (rel == 1), (3, 2), 2)
+    send_lights((pos == 1) & (rel == 1), (2,), 2)
     send_lights((pos == 1) & (rel == 2), (3, 1), 2)
     relay((2, 2))
     relay((2, 3), (3, 0))

time: 55.1 us -> 54.6 us (level)
  no operation moved by 1% of the time
where the time goes in v7:
time: 54.6 us; the launch traced here: 54.4 us
  Pallas kernels  51.7 us (95%)
  between operations  1.63 us (3%)
  loops' own time  0.55 us (1%)
    pallas_call x1, Pallas kernels, run(): call(act, act_part, gain, wq, wk, wv, wo, chip_k, chip_v, twist, tokens,...  38.2 us
    pallas_call x1, Pallas kernels, adaptive(): pl.pallas_call(functools.partial(plan_kernel, parts, doms, tps, cap, HOT_...  11.5 us
    pallas_call x1, Pallas kernels, adaptive(): pl.pallas_call(functools.partial(finish_kernel, parts, steps), out_shape=...  1.99 us

profile of v7, /device:TPU:0, one launch (start us, length us, event | category | flops | bytes accessed | tf_op | source)
XLA Modules:
  0.0 54.4 jit_solution(14952826231343267877)
XLA Ops:
  0.6 0.0 copy-start.8
  0.6 0.0 copy-start.7
  0.7 0.0 copy-start.6
  0.7 0.0 copy-start.2
  0.7 0.0 copy-start.5
  0.7 0.0 copy-start.4
  0.7 0.0 copy-start.3
  0.7 11.5 %plan.1 = (s32[8,128]{1,0:T(8,128)S(1)}, bf16[32,128,256]{2,1,0:T(8,128)(2,1)S(1)}, bf16[32,128,256]{2,1,0:T(8,128)(2,1)S(1)}, bf16[4,16,1024]{2,1,0:T(8,128)(2,1)S(1)}) custom-call(s32[1,16]{1,0:T(1,128)} %bitcast.45, bf16[64,1024]{1,0:T(8,128)(2,1)} %bitcast.25, bf16[16,128,256]{2,1,0:T(8,128)(2,1)} %ck.1, bf16[16,128,256]{2,1,0:T(8,128)(2,1)} %cv.1), custom_call_target="tpu_custom_call" | custom-call | tf_op jit(solution)/shard_map/plan/pallas_call | solution.py:1214
  12.2 0.5 slice.3
  13.3 0.0 copy-done.8
  13.4 0.0 copy-done.7
  13.4 0.0 copy-done.6
  13.4 0.0 copy-done.2
  13.4 0.0 copy-done.5
  13.4 0.0 copy-done.4
  13.4 0.0 copy-done.3
  13.4 38.8 %conditional.1 = (bf16[16,128,256]{2,1,0:T(8,128)(2,1)S(1)}, bf16[16,128,256]{2,1,0:T(8,128)(2,1)S(1)}, bf16[64,1024]{1,0:T(8,128)(2,1)S(1)}, bf16[128,512]{1,0:T(8,128)(2,1)S(1)}, f32[1,16]{1,0:T(1,128)S(1)}) conditional(s32[]{:T(128)} %bitcast.12, (bf16[128256]{0:T(1024)(128)(2,1)}, f32[16]{0:T(128)S(1)}, ...), branch_computations={%region_0.0_spmd, %region_1.0_spmd, %region_2.0_spmd, %region_3.0_... | conditional | flops 1328 | bytes 67116392 | solution.py:1302
  13.4 38.2 %main0.1 = (bf16[64,1024]{1,0:T(8,128)(2,1)S(1)}, bf16[16,128,256]{2,1,0:T(8,128)(2,1)S(1)}, bf16[16,128,256]{2,1,0:T(8,128)(2,1)S(1)}, bf16[128,512]{1,0:T(8,128)(2,1)S(1)}, f32[1,16]{1,0:T(1,128)S(1)}) custom-call(bf16[64,1024]{1,0:T(8,128)(2,1)S(1)} %get-tuple-element.166.act, bf16[4,16,1024]{2,1,0:T(8,128)(2,1)S(1)} %get-tuple-element.167.act_part, ...), custom_call_target="tpu_custom_call" | custom-call | tf_op jit(solution)/shard_map/cond/branch_0_fun/main0/pallas_call | solution.py:1283
  52.2 2.0 %finish.1 = (bf16[132,16,256]{2,1,0:T(8,128)(2,1)}, bf16[132,16,256]{2,1,0:T(8,128)(2,1)}, bf16[64,1024]{1,0:T(8,128)(2,1)}, f32[1,16]{1,0:T(1,128)}) custom-call(bf16[16,128,256]{2,1,0:T(8,128)(2,1)S(1)} %get-tuple-element.297.rows_k, bf16[16,128,256]{2,1,0:T(8,128)(2,1)S(1)} %get-tuple-element.298.rows_v, bf16[128,512]{1,0:T(8,128)(2,1)S(1)} %get-tuple-element.299.chosen, ...), custom_call_target="tpu_custom_call" | custom-call | tf_op jit(solution)/shard_map/finish/pallas_call | solution.py:1311
Async XLA Ops:
  0.6 12.7 %copy-start.8 = (s32[16]{0:T(128)S(1)}, s32[16]{0:T(128)}, u32[]{:S(2)}) copy-start(s32[16]{0:T(128)} %param.32) | copy-start | bytes 196
  0.6 12.7 %copy-start.7 = (f32[16]{0:T(128)S(1)}, f32[16]{0:T(128)}, u32[]{:S(2)}) copy-start(f32[16]{0:T(128)} %param.31) | copy-start | bytes 196
  0.7 12.7 %copy-start.6 = (s32[4,16]{1,0:T(4,128)S(1)}, s32[4,16]{1,0:T(4,128)}, u32[]{:S(2)}) copy-start(s32[4,16]{1,0:T(4,128)} %param.28) | copy-start | bytes 772
  0.7 12.7 %copy-start.2 = (bf16[4096,256]{1,0:T(8,128)(2,1)S(1)}, bf16[4096,256]{1,0:T(8,128)(2,1)}, u32[]{:S(2)}) copy-start(bf16[4096,256]{1,0:T(8,128)(2,1)} %param.23) | copy-start | bytes 6291460
  0.7 12.7 %copy-start.5 = (f32[1024]{0:T(1024)S(1)}, f32[1024]{0:T(1024)}, u32[]{:S(2)}) copy-start(f32[1024]{0:T(1024)} %param.30) | copy-start | bytes 12292
  0.7 12.7 %copy-start.4 = (f32[4096]{0:T(1024)S(1)}, f32[4096]{0:T(1024)}, u32[]{:S(2)}) copy-start(f32[4096]{0:T(1024)} %param.21) | copy-start | bytes 49156
  0.7 12.7 %copy-start.3 = (bf16[4,16,1024]{2,1,0:T(8,128)(2,1)S(1)}, bf16[4,16,1024]{2,1,0:T(8,128)(2,1)}, u32[]{:S(2)}) copy-start(bf16[4,16,1024]{2,1,0:T(8,128)(2,1)} %param.20) | copy-start | bytes 393220
